TPU v7x, 32 devices: a 4x2x2 block of a 4x4x8 slice. The times are simulated.
32 devices in a mesh: dp: 4 (over y, z), sp: 8 (over x, core).
Axes of the slice: x: 4, y: 2, z: 2, core: 2. Of those that a mesh axis runs over, the one named last changes fastest.
The devices are a block of a 4x4x8 slice.
Arguments:
- tokens: bfloat16 [32, 16, 64, 1152], P('dp', 'sp'), parts along dimension 0
- caption: bfloat16 [32, 120, 1152], P('dp'), parts along dimension 0
- cap_valid: int32 [32, 120], P('dp'), parts along dimension 0
- time_emb: bfloat16 [32, 6912], P('dp'), parts along dimension 0
- ada_table: bfloat16 [2, 6, 1152], replicated
- attn_wq: bfloat16 [2, 1152, 1152], replicated
- attn_bq: bfloat16 [2, 1152], replicated
- attn_wkv: bfloat16 [2, 1152, 2304], replicated
- attn_bkv: bfloat16 [2, 2304], replicated
- attn_wo: bfloat16 [2, 1152, 1152], replicated
- attn_bo: bfloat16 [2, 1152], replicated
- comp_w: bfloat16 [2, 2, 1152], replicated
- comp_b: bfloat16 [1152], replicated
- cnorm_g: bfloat16 [1152], replicated
- cnorm_b: bfloat16 [1152], replicated
- cross_wq: bfloat16 [2, 1152, 1152], replicated
- cross_bq: bfloat16 [2, 1152], replicated
- cross_wkv: bfloat16 [2, 1152, 2304], replicated
- cross_bkv: bfloat16 [2, 2304], replicated
- cross_wo: bfloat16 [2, 1152, 1152], replicated
- cross_bo: bfloat16 [2, 1152], replicated
- mlp_w1: bfloat16 [2, 1152, 4608], replicated
- mlp_b1: bfloat16 [2, 4608], replicated
- mlp_w2: bfloat16 [2, 4608, 1152], replicated
- mlp_b2: bfloat16 [2, 1152], replicated
Outputs:
- output: bfloat16 [32, 16, 64, 1152], P('dp', 'sp'), parts along dimension 0
There are 4 independent parts. A program takes and returns all parts, laid end to end along the dimension named above; an argument that names none is the same for every part.
All inputs are finite; a program needn't handle non-finite values.
Results may differ from a plain program's by a relative error of at most 0.0163797.
Values are sent between devices in bfloat16 or wider.
A program may use at most 768 MiB of HBM per device.

v0:
```python
import math
import jax
import jax.numpy as jnp
from jax import lax
from jax.sharding import PartitionSpec as P

HEAD_DIM = 72
LN_EPS = 1e-6


def layer_norm(values):
    row_mean = jnp.mean(values, axis=-1, keepdims=True)
    centered = values - row_mean
    variance = jnp.mean(centered * centered, axis=-1, keepdims=True)
    return centered * lax.rsqrt(variance + LN_EPS)


def linear(activations, weight, bias_vec):
    return jnp.dot(activations, weight, preferred_element_type=jnp.float32) + bias_vec.astype(jnp.float32)


def modulations(time_emb, table_row):
    mods = time_emb.astype(jnp.float32).reshape(time_emb.shape[0], 6, -1) + table_row.astype(jnp.float32)[None]
    return mods[:, :, None, None, :]


def compress(mod_in, conv_w, conv_b, norm_g, norm_b):
    num_batch, num_rows, grid_w, model_dim = mod_in.shape
    grid_view = mod_in.reshape(num_batch, num_rows // 2, 2, grid_w // 2, 2, model_dim).astype(jnp.float32)
    conv_sum = jnp.sum(grid_view * conv_w.astype(jnp.float32)[:, None, :, :], axis=(2, 4)) + conv_b.astype(jnp.float32)
    return (layer_norm(conv_sum) * norm_g.astype(jnp.float32) + norm_b.astype(jnp.float32)).astype(jnp.bfloat16)


def attend(queries, keys_in, values_in, key_bias):
    num_batch, num_query, model_dim = queries.shape
    num_heads = model_dim // HEAD_DIM
    blk_size = math.gcd(num_query, 128)
    query_blocks = jnp.moveaxis(queries.reshape(num_batch, num_query // blk_size, blk_size, num_heads, HEAD_DIM), 1, 0)
    key_heads = keys_in.reshape(num_batch, -1, num_heads, HEAD_DIM)
    value_heads = values_in.reshape(num_batch, -1, num_heads, HEAD_DIM)

    def one_block(query_blk):
        scores = jnp.einsum('bqhd,bkhd->bhqk', query_blk, key_heads, preferred_element_type=jnp.float32) * (HEAD_DIM ** -0.5)
        if key_bias is not None:
            scores = scores + key_bias[:, None, None, :]
        attn_probs = jax.nn.softmax(scores, axis=-1).astype(jnp.bfloat16)
        return jnp.einsum('bhqk,bkhd->bqhd', attn_probs, value_heads, preferred_element_type=jnp.float32).astype(jnp.bfloat16)

    out_blocks = lax.map(one_block, query_blocks)
    return jnp.moveaxis(out_blocks, 0, 1).reshape(num_batch, num_query, model_dim)


def solution(mesh):
    in_specs = (P('dp', 'sp', None, None), P('dp', None, None), P('dp', None), P('dp', None)) + (P(),) * 21
    out_specs = P('dp', 'sp', None, None)

    def device_fn(tokens, caption, cap_valid, time_emb, ada_table, attn_wq, attn_bq, attn_wkv, attn_bkv, attn_wo, attn_bo, comp_w, comp_b, cnorm_g, cnorm_b, cross_wq, cross_bq, cross_wkv, cross_bkv, cross_wo, cross_bo, mlp_w1, mlp_b1, mlp_w2, mlp_b2):
        num_batch = tokens.shape[0]
        model_dim = tokens.shape[3]
        key_bias = jnp.where(cap_valid > 0, 0.0, -1e9).astype(jnp.float32)
        hidden = tokens
        for layer_idx in range(2):
            mods = modulations(time_emb, ada_table[layer_idx])
            mod_in = (layer_norm(hidden.astype(jnp.float32)) * (1.0 + mods[:, 1]) + mods[:, 0]).astype(jnp.bfloat16)
            queries = linear(mod_in, attn_wq[layer_idx], attn_bq[layer_idx]).astype(jnp.bfloat16).reshape(num_batch, -1, model_dim)
            kv_src = compress(mod_in, comp_w, comp_b, cnorm_g, cnorm_b) if layer_idx == 0 else mod_in
            local_kv = linear(kv_src, attn_wkv[layer_idx], attn_bkv[layer_idx]).astype(jnp.bfloat16).reshape(num_batch, -1, 2 * model_dim)
            key_vals = lax.all_gather(local_kv, 'sp', axis=1, tiled=True)
            attn_out = attend(queries, key_vals[:, :, :model_dim], key_vals[:, :, model_dim:], None)
            attn_proj = linear(attn_out, attn_wo[layer_idx], attn_bo[layer_idx]).reshape(hidden.shape)
            hidden = (hidden.astype(jnp.float32) + mods[:, 2] * attn_proj).astype(jnp.bfloat16)
            cross_q = linear(hidden, cross_wq[layer_idx], cross_bq[layer_idx]).astype(jnp.bfloat16).reshape(num_batch, -1, model_dim)
            cross_kv = linear(caption, cross_wkv[layer_idx], cross_bkv[layer_idx]).astype(jnp.bfloat16)
            cross_out = attend(cross_q, cross_kv[:, :, :model_dim], cross_kv[:, :, model_dim:], key_bias)
            cross_proj = linear(cross_out, cross_wo[layer_idx], cross_bo[layer_idx]).reshape(hidden.shape)
            hidden = (hidden.astype(jnp.float32) + cross_proj).astype(jnp.bfloat16)
            mlp_in = (layer_norm(hidden.astype(jnp.float32)) * (1.0 + mods[:, 4]) + mods[:, 3]).astype(jnp.bfloat16)
            mlp_act = jax.nn.gelu(linear(mlp_in, mlp_w1[layer_idx], mlp_b1[layer_idx]), approximate=True).astype(jnp.bfloat16)
            mlp_out = linear(mlp_act, mlp_w2[layer_idx], mlp_b2[layer_idx])
            hidden = (hidden.astype(jnp.float32) + mods[:, 5] * mlp_out).astype(jnp.bfloat16)
        return hidden

    return jax.shard_map(device_fn, mesh=mesh, in_specs=in_specs, out_specs=out_specs, check_vma=False)
```

profile of v0, /device:TPU:81, one launch (start us, length us, event | category | flops | bytes accessed | tf_op | source)
XLA Modules:
  0.0 665.1 jit_solution(13186776139393656417)
XLA Ops:
  6.6 1.0 fusion.208
  7.6 1.7 convert_add_fusion.4
  9.3 0.6 slice_bitcast_fusion.5
  9.9 2.0 convert_reduce_fusion.3
  12.0 0.8 fusion.89
  13.5 4.6 multiply_reduce_fusion.2
  18.1 1.4 bitcast_reduce_fusion
  20.1 0.6 convert_reduce_fusion.7
  20.7 2.9 fusion.120
  24.4 7.6 %add_convert_fusion.8 = bf16[8,2,64,1152]{3,2,1,0:T(8,128)(2,1)} fusion(bf16[2,1152,1152]{2,1,0:T(8,128)(2,1)} %param.30, f32[1152]{0:T(1024)S(1)} %get-tuple-element.78, bf16[8,2,64,1152]{3,2,1,0:T(8,128)(2,1)} %param.25, f32[8,1152]{1,0:T(8,128)S(1)} %get-tuple-element.108, f32[8,1152]{1,0:T(8,128)S(1)} %get-tuple-element.109, ...), kind=kOutput, calls=%fused_computation.120 | convolution fusion | flops 2727346176 | bytes 7459328 | tf_op jit(solution)/shard_map/dot_general | solution.py:19
  32.0 10.1 %squeeze.97 = bf16[8,128,16,72]{3,2,1,0:T(8,128)(2,1)} reshape(bf16[8,2,64,1152]{3,2,1,0:T(8,128)(2,1)} %add_convert_fusion.8) | data formatting | bytes 4718592 | tf_op jit(solution)/shard_map/while/body/jit(dynamic_index_in_dim)/squeeze | solution.py:49
  42.2 0.6 convert_reduce_fusion.8
  42.8 8.6 %add_convert_fusion.2 = bf16[8,120,2304]{2,1,0:T(8,128)(2,1)S(1)} fusion(bf16[8,120,1152]{2,1,0:T(8,128)(2,1)S(1)} %copy-done, bf16[2,1152,2304]{2,1,0:T(8,128)(2,1)} %param.42, f32[2304]{0:T(1024)S(1)} %get-tuple-element.56), kind=kOutput, calls=%fused_computation.54 | convolution fusion | flops 5100503040 | bytes 11953152 | tf_op jit(solution)/shard_map/dot_general | solution.py:19
  51.4 2.4 fusion.206
  53.9 4.4 copy.114
  58.2 4.2 copy.113
  65.0 0.7 convert_reduce_fusion.4
  65.6 0.7 slice_bitcast_fusion.1
  66.4 12.9 %all-gather.3.cloned.1.call-done = bf16[8,256,2304]{2,1,0:T(8,128)(2,1)} async-done(((bf16[8,32,2304]{2,1,0:T(8,128)(2,1)}), bf16[8,256,2304]{2,1,0:T(8,128)(2,1)}) %all-gather.3.cloned.1.call-update) | async-done | bytes 9437200 | tf_op jit(solution)/shard_map/all_gather | solution.py:68
  79.3 8.4 %fusion.205 = (bf16[8,256,1152]{2,1,0:T(8,128)(2,1)}, bf16[8,256,1152]{2,1,0:T(8,128)(2,1)}) fusion(bf16[8,256,2304]{2,1,0:T(8,128)(2,1)} %all-gather.3.cloned.1.call-done), kind=kLoop, calls=%fused_computation.245 | loop fusion | bytes 18874368 | tf_op jit(solution)/shard_map/slice | solution.py:69
  87.7 6.6 copy.110
  94.3 11.7 %fusion.109 = f32[8,16,128,256]{3,2,1,0:T(8,128)} fusion(bf16[8,256,16,72]{1,3,2,0:T(8,128)(2,1)} %bitcast.219, bf16[8,128,16,72]{3,2,1,0:T(8,128)(2,1)} %squeeze.97), kind=kOutput, calls=%fused_computation.130 | convolution fusion | flops 603979776 | bytes 23855104 | tf_op jit(solution)/shard_map/while/body/eval_jaxpr/bqhd,bkhd->bhqk/dot_general | solution.py:43
  105.9 16.0 %fusion.209 = f32[8,16,128]{2,1,0:T(8,128)S(1)} fusion(f32[8,16,128,256]{3,2,1,0:T(8,128)} %fusion.109), kind=kOutput, calls=%fused_computation.249 | output fusion | flops 16777472 | bytes 16842752 | tf_op jit(solution)/shard_map/while/body/eval_jaxpr/sub | solution.py:46
  122.0 6.6 copy.109
  128.6 41.7 %fusion.168 = bf16[8,16,72,128]{3,2,1,0:T(8,128)(2,1)} fusion(bf16[8,256,16,72]{1,3,2,0:T(8,128)(2,1)} %bitcast.226, f32[8,16,128]{2,1,0:T(8,128)S(1)} %fusion.209, f32[8,16,128,256]{3,2,1,0:T(8,128)} %fusion.109), kind=kOutput, calls=%fused_computation.170 | convolution fusion | flops 626147584 | bytes 23920640 | tf_op jit(solution)/shard_map/while/body/eval_jaxpr/bhqk,bkhd->bqhd/dot_general | solution.py:47
  170.3 6.2 convolution_add_fusion.3
  176.5 0.7 fusion.93
  177.3 1.4 copy-done.8
  178.7 6.5 add_convert_fusion.7
  185.2 9.6 %squeeze.101 = bf16[8,128,16,72]{3,2,1,0:T(8,128)(2,1)} reshape(bf16[8,2,64,1152]{3,2,1,0:T(8,128)(2,1)} %add_convert_fusion.7) | data formatting | bytes 4718592 | tf_op jit(solution)/shard_map/while/body/jit(dynamic_index_in_dim)/squeeze | solution.py:49
  194.8 5.3 fusion.107
  200.2 3.4 fusion.210
  203.5 1.6 fusion.167
  205.1 5.5 convolution_add_fusion.2
  211.3 0.8 fusion.85
  212.1 21.2 %fusion.16.clone.3.clone.5 = bf16[8,2,64,4608]{3,2,1,0:T(8,128)(2,1)} fusion(bf16[2,1152,4608]{2,1,0:T(8,128)(2,1)} %param.46, f32[4608]{0:T(1024)S(1)} %get-tuple-element.48, bf16[8,2,64,1152]{3,2,1,0:T(8,128)(2,1)S(1)} %get-tuple-element.88, f32[8,1152]{1,0:T(8,128)S(1)} %get-tuple-element.106, ...), kind=kOutput, calls=%fused_computation.19.clone.clone.clone.clone.clone.clone.clone.2 | convolution fusion | flops 10925899776 | bytes 22513664 | tf_op jit(solution)/shard_map/dot_general | solution.py:19
  233.4 18.3 %convert_reduce_fusion.1 = (f32[8,2,64]{2,1,0:T(2,128)S(1)}, bf16[8,2,64,1152]{3,2,1,0:T(8,128)(2,1)S(1)}) fusion(f32[1152]{0:T(1024)S(1)} %copy-done.40, bf16[2,4608,1152]{2,1,0:T(8,128)(2,1)} %param.48, bf16[8,2,64,1152]{3,2,1,0:T(8,128)(2,1)S(1)} %get-tuple-element.88, f32[8,1152]{1,0:T(8,128)S(1)} %copy-done.20, ...), kind=kOutput, calls=%fused_computation.68 | convolution fusion | flops 10879892480 | bytes 24818176 | tf_op jit(solution)/shard_map/dot_general | solution.py:19
  251.7 0.8 fusion.81
  252.5 11.1 %add_convert_fusion = bf16[8,2,64,2304]{3,2,1,0:T(8,128)(2,1)} fusion(bf16[2,1152,2304]{2,1,0:T(8,128)(2,1)} %param.32, f32[2304]{0:T(1024)S(1)} %copy-done.32, bf16[8,2,64,1152]{3,2,1,0:T(8,128)(2,1)S(1)} %get-tuple-element.118, f32[8,1152]{1,0:T(8,128)S(1)} %copy-done.22, f32[8,1152]{1,0:T(8,128)S(1)} %copy-done.23, f32[8,2,64]{2,1,0:T(2,128)S(1)} %add_rsqrt_fusion.1, ...), kind=kOutput, calls=%fused_computation.43 | convolution fusion | flops 5447614464 | bytes 12477440 | tf_op jit(solution)/shard_map/dot_general | solution.py:19
  263.7 0.6 copy-done.33
  264.3 8.6 %add_convert_fusion.1 = bf16[8,120,2304]{2,1,0:T(8,128)(2,1)S(1)} fusion(bf16[8,120,1152]{2,1,0:T(8,128)(2,1)S(1)} %copy-done, bf16[2,1152,2304]{2,1,0:T(8,128)(2,1)} %param.42, f32[2304]{0:T(1024)S(1)} %copy-done.33), kind=kOutput, calls=%fused_computation.53 | convolution fusion | flops 5100503040 | bytes 11953152 | tf_op jit(solution)/shard_map/dot_general | solution.py:19
  272.9 1.7 fusion.207
  274.6 4.3 copy.124
  278.9 2.5 copy.123
  281.4 7.6 %add_convert_fusion.5 = bf16[8,2,64,1152]{3,2,1,0:T(8,128)(2,1)} fusion(bf16[2,1152,1152]{2,1,0:T(8,128)(2,1)} %param.30, f32[1152]{0:T(1024)S(1)} %copy-done.39, bf16[8,2,64,1152]{3,2,1,0:T(8,128)(2,1)} %copy-done.4, f32[8,1152]{1,0:T(8,128)S(1)} %copy-done.22, f32[8,1152]{1,0:T(8,128)S(1)} %copy-done.23, f32[8,2,64]{2,1,0:T(2,128)S(1)} %add_rsqrt_fusion.1, ...), kind=kOutput, calls=%fused_computation.117 | convolution fusion | flops 2727346176 | bytes 7459328 | tf_op jit(solution)/shard_map/dot_general | solution.py:19
  289.0 9.6 %squeeze.107 = bf16[8,128,16,72]{3,2,1,0:T(8,128)(2,1)} reshape(bf16[8,2,64,1152]{3,2,1,0:T(8,128)(2,1)} %add_convert_fusion.5) | data formatting | bytes 4718592 | tf_op jit(solution)/shard_map/while/body/jit(dynamic_index_in_dim)/squeeze | solution.py:49
  298.6 138.3 %all-gather.5.cloned.1.call-done = bf16[8,1024,2304]{2,1,0:T(8,128)(2,1)} async-done(((bf16[8,128,2304]{2,1,0:T(8,128)(2,1)}), bf16[8,1024,2304]{2,1,0:T(8,128)(2,1)}) %all-gather.5.cloned.1.call-update) | async-done | bytes 37748752 | tf_op jit(solution)/shard_map/all_gather | solution.py:68
  436.9 25.5 %fusion.204 = (bf16[8,1024,1152]{2,1,0:T(8,128)(2,1)}, bf16[8,1024,1152]{2,1,0:T(8,128)(2,1)}) fusion(bf16[8,1024,2304]{2,1,0:T(8,128)(2,1)} %all-gather.5.cloned.1.call-done), kind=kLoop, calls=%fused_computation.244 | loop fusion | bytes 75497472 | tf_op jit(solution)/shard_map/slice | solution.py:69
  462.4 24.6 %copy.120 = bf16[8,1024,1152]{1,2,0:T(8,128)(2,1)} copy(bf16[8,1024,1152]{2,1,0:T(8,128)(2,1)} %get-tuple-element.90) | data formatting | bytes 37748736 | tf_op jit(solution)/shard_map/slice | solution.py:69
  487.1 24.7 %copy.119 = bf16[8,1024,1152]{1,2,0:T(8,128)(2,1)} copy(bf16[8,1024,1152]{2,1,0:T(8,128)(2,1)} %get-tuple-element.92) | data formatting | bytes 37748736 | tf_op jit(solution)/shard_map/slice | solution.py:69
  511.8 37.0 %fusion.215 = (f32[8,16,128]{2,1,0:T(8,128)S(1)}, f32[8,16,128,1024]{3,2,1,0:T(8,128)}) fusion(bf16[8,1024,16,72]{1,3,2,0:T(8,128)(2,1)} %bitcast.220, bf16[8,128,16,72]{3,2,1,0:T(8,128)(2,1)} %squeeze.107), kind=kOutput, calls=%fused_computation.251 | convolution fusion | flops 2466251776 | bytes 88408064 | tf_op jit(solution)/shard_map/while/body/eval_jaxpr/sub | solution.py:46
  548.7 30.4 %fusion.169 = bf16[8,16,72,128]{3,2,1,0:T(8,128)(2,1)} fusion(bf16[8,1024,16,72]{1,3,2,0:T(8,128)(2,1)} %bitcast.221, f32[8,16,128,1024]{3,2,1,0:T(8,128)} %get-tuple-element.120, f32[8,16,128]{2,1,0:T(8,128)S(1)} %get-tuple-element.119), kind=kOutput, calls=%fused_computation.171 | convolution fusion | flops 2450653184 | bytes 88408064 | tf_op jit(solution)/shard_map/while/body/eval_jaxpr/bhqk,bkhd->bqhd/dot_general | solution.py:47
  579.1 6.2 convolution_add_fusion.1
  585.4 0.7 fusion.95
  586.2 1.4 copy-done.6
  587.6 6.5 add_convert_fusion.4
  594.1 10.0 %squeeze.111 = bf16[8,128,16,72]{3,2,1,0:T(8,128)(2,1)} reshape(bf16[8,2,64,1152]{3,2,1,0:T(8,128)(2,1)} %add_convert_fusion.4) | data formatting | bytes 4718592 | tf_op jit(solution)/shard_map/while/body/jit(dynamic_index_in_dim)/squeeze | solution.py:49
  604.1 5.3 fusion.105
  609.4 3.1 fusion.220
  612.6 1.6 fusion.166
  614.2 5.5 convolution_add_fusion
  620.3 0.8 fusion.77
  621.2 18.8 %fusion.24.clone.7 = bf16[8,2,64,4608]{3,2,1,0:T(8,128)(2,1)S(1)} fusion(bf16[2,1152,4608]{2,1,0:T(8,128)(2,1)} %param.46, f32[4608]{0:T(1024)S(1)} %copy-done.26, bf16[8,2,64,1152]{3,2,1,0:T(8,128)(2,1)S(1)} %get-tuple-element.80, f32[8,1152]{1,0:T(8,128)S(1)} %copy-done.18, f32[8,1152]{1,0:T(8,128)S(1)} %copy-done.19, ...), kind=kOutput, calls=%fused_computation.27.clone.clone.clone.clone.clone.2 | convolution fusion | flops 10925899776 | bytes 22513664 | tf_op jit(solution)/shard_map/dot_general | solution.py:19
  640.0 18.1 %fusion.96 = bf16[8,2,64,1152]{3,2,1,0:T(8,128)(2,1)} fusion(bf16[8,2,64,1152]{3,2,1,0:T(8,128)(2,1)S(1)} %get-tuple-element.80, bf16[2,4608,1152]{2,1,0:T(8,128)(2,1)} %param.48, f32[1152]{0:T(1024)S(1)} %copy-done.35, f32[8,1152]{1,0:T(8,128)S(1)} %copy-done.17, bf16[8,2,64,4608]{3,2,1,0:T(8,128)(2,1)S(1)} %fusion.24.clone.7), kind=kOutput, calls=%fused_computation.114 | convolution fusion | flops 10877534208 | bytes 24814080 | tf_op jit(solution)/shard_map/dot_general | solution.py:19
  (119 shorter events, 6.0 us)
Async XLA Ops:
  6.5 36.3 %copy-start = (bf16[8,120,1152]{2,1,0:T(8,128)(2,1)S(1)}, bf16[8,120,1152]{2,1,0:T(8,128)(2,1)}, u32[]{:S(2)}) copy-start(bf16[8,120,1152]{2,1,0:T(8,128)(2,1)} %param.26) | copy-start | bytes 6635524
  6.6 6.3 copy-start.34
  6.6 72.8 %all-gather.3.cloned.1.call-start = ((), (), s32[]{:S(2)}) async-start(), calls=%async_computation | async-start | bytes 10616832 | tf_op jit(solution)/shard_map/all_gather | solution.py:68
  6.6 5.4 copy-start.2
  13.4 6.0 copy-start.41
  13.4 6.6 copy-start.24
  13.4 7.3 %copy-start.42 = (bf16[1152]{0:T(1024)(128)(2,1)S(1)}, bf16[1152]{0:T(1024)(128)(2,1)}, u32[]{:S(2)}) copy-start(bf16[1152]{0:T(1024)(128)(2,1)} %param.38) | copy-start | bytes 6916
  13.4 7.3 %copy-start.43 = (bf16[1152]{0:T(1024)(128)(2,1)S(1)}, bf16[1152]{0:T(1024)(128)(2,1)}, u32[]{:S(2)}) copy-start(bf16[1152]{0:T(1024)(128)(2,1)} %param.39) | copy-start | bytes 6916
  13.4 7.3 %copy-start.45 = (bf16[2,1152,2304]{2,1,0:T(8,128)(2,1)S(1)}, bf16[2,1152,2304]{2,1,0:T(8,128)(2,1)}, u32[]{:S(2)}) copy-start(bf16[2,1152,2304]{2,1,0:T(8,128)(2,1)} %param.32) | copy-start | bytes 31850500
  20.7 3.1 copy-start.27
  23.7 413.2 %all-gather.5.cloned.1.call-start = ((), (), s32[]{:S(2)}) async-start(), calls=%async_computation.1 | async-start | bytes 42467328 | tf_op jit(solution)/shard_map/all_gather | solution.py:68
  32.0 10.1 %copy-start.25 = (bf16[2,2304]{1,0:T(2,128)(2,1)S(1)}, bf16[2,2304]{1,0:T(2,128)(2,1)}, u32[]{:S(2)}) copy-start(bf16[2,2304]{1,0:T(2,128)(2,1)} %param.43) | copy-start | bytes 27652
  53.9 8.6 %copy-start.28 = (bf16[2,1152]{1,0:T(2,128)(2,1)S(1)}, bf16[2,1152]{1,0:T(2,128)(2,1)}, u32[]{:S(2)}) copy-start(bf16[2,1152]{1,0:T(2,128)(2,1)} %param.35) | copy-start | bytes 13828
  53.9 9.2 %copy-start.29 = (bf16[2,1152]{1,0:T(2,128)(2,1)S(1)}, bf16[2,1152]{1,0:T(2,128)(2,1)}, u32[]{:S(2)}) copy-start(bf16[2,1152]{1,0:T(2,128)(2,1)} %param.41) | copy-start | bytes 13828
  53.9 9.9 %copy-start.30 = (bf16[2,1152]{1,0:T(2,128)(2,1)S(1)}, bf16[2,1152]{1,0:T(2,128)(2,1)}, u32[]{:S(2)}) copy-start(bf16[2,1152]{1,0:T(2,128)(2,1)} %param.45) | copy-start | bytes 13828
  53.9 10.5 %copy-start.31 = (bf16[2,1152]{1,0:T(2,128)(2,1)S(1)}, bf16[2,1152]{1,0:T(2,128)(2,1)}, u32[]{:S(2)}) copy-start(bf16[2,1152]{1,0:T(2,128)(2,1)} %param.49) | copy-start | bytes 13828
  53.9 11.1 %copy-start.14 = (bf16[2,4608]{1,0:T(2,128)(2,1)S(1)}, bf16[2,4608]{1,0:T(2,128)(2,1)}, u32[]{:S(2)}) copy-start(bf16[2,4608]{1,0:T(2,128)(2,1)} %param.47) | copy-start | bytes 55300
  53.9 11.7 %copy-start.44 = (s32[8,120]{1,0:T(8,128)S(1)}, s32[8,120]{1,0:T(8,128)}, u32[]{:S(2)}) copy-start(s32[8,120]{1,0:T(8,128)} %param.27) | copy-start | bytes 11524
  53.9 11.7 %copy-start.12 = (f32[8,6,1,1,1152]{4,0,3,2,1:T(8,128)S(1)}, f32[8,6,1,1,1152]{4,0,3,2,1:T(8,128)}, u32[]{:S(2)}) copy-start(f32[8,6,1,1,1152]{4,0,3,2,1:T(8,128)} %get-tuple-element.111) | copy-start | bytes 663556
  65.6 134.5 %copy-start.15 = (f32[8,120]{1,0:T(8,128)}, f32[8,120]{1,0:T(8,128)S(1)}, u32[]{:S(2)}) copy-start(f32[8,120]{1,0:T(8,128)S(1)} %compare_select_fusion) | copy-start | bytes 11524
  170.3 6.2 copy-start.3
  177.3 1.4 copy-start.8
  200.2 3.4 copy-start.10
  205.1 5.5 copy-start.9
  210.7 1.4 copy-start.21
  212.1 21.3 %copy-start.20 = (f32[8,1152]{1,0:T(8,128)S(1)}, f32[8,1152]{1,0:T(8,128)}, u32[]{:S(2)}) copy-start(f32[8,1152]{1,0:T(8,128)} %get-tuple-element.105) | copy-start | bytes 110596
  212.1 21.3 %copy-start.40 = (f32[1152]{0:T(1024)S(1)}, f32[1152]{0:T(1024)}, u32[]{:S(2)}) copy-start(f32[1152]{0:T(1024)} %get-tuple-element.64) | copy-start | bytes 13828
  233.4 19.1 %copy-start.22 = (f32[8,1152]{1,0:T(8,128)S(1)}, f32[8,1152]{1,0:T(8,128)}, u32[]{:S(2)}) copy-start(f32[8,1152]{1,0:T(8,128)} %get-tuple-element.102) | copy-start | bytes 110596
  233.4 19.1 %copy-start.23 = (f32[8,1152]{1,0:T(8,128)S(1)}, f32[8,1152]{1,0:T(8,128)}, u32[]{:S(2)}) copy-start(f32[8,1152]{1,0:T(8,128)} %get-tuple-element.103) | copy-start | bytes 110596
  233.4 19.1 %copy-start.32 = (f32[2304]{0:T(1024)S(1)}, f32[2304]{0:T(1024)}, u32[]{:S(2)}) copy-start(f32[2304]{0:T(1024)} %get-tuple-element.54) | copy-start | bytes 27652
  251.7 11.9 %copy-start.4 = (bf16[8,2,64,1152]{3,2,1,0:T(8,128)(2,1)}, bf16[8,2,64,1152]{3,2,1,0:T(8,128)(2,1)S(1)}, u32[]{:S(2)}) copy-start(bf16[8,2,64,1152]{3,2,1,0:T(8,128)(2,1)S(1)} %get-tuple-element.118) | copy-start | bytes 7077892
  263.6 0.7 copy-start.33
  274.6 6.7 %copy-start.39 = (f32[1152]{0:T(1024)S(1)}, f32[1152]{0:T(1024)}, u32[]{:S(2)}) copy-start(f32[1152]{0:T(1024)} %get-tuple-element.77) | copy-start | bytes 13828
  548.7 30.4 %copy-start.38 = (f32[1152]{0:T(1024)S(1)}, f32[1152]{0:T(1024)}, u32[]{:S(2)}) copy-start(f32[1152]{0:T(1024)} %get-tuple-element.69) | copy-start | bytes 13828
  579.1 6.2 copy-start.5
  579.1 6.2 copy-start.13
  585.4 2.2 copy-start.37
  586.1 1.4 copy-start.6
  604.1 5.3 copy-start.16
  609.4 3.1 copy-start.11
  612.5 1.6 copy-start.36
  614.2 5.5 copy-start.7
  619.7 1.5 copy-start.18
  619.7 1.5 copy-start.19
  619.7 1.5 copy-start.26
  621.2 18.8 %copy-start.17 = (f32[8,1152]{1,0:T(8,128)S(1)}, f32[8,1152]{1,0:T(8,128)}, u32[]{:S(2)}) copy-start(f32[8,1152]{1,0:T(8,128)} %get-tuple-element.99) | copy-start | bytes 110596
  621.2 18.8 %copy-start.35 = (f32[1152]{0:T(1024)S(1)}, f32[1152]{0:T(1024)}, u32[]{:S(2)}) copy-start(f32[1152]{0:T(1024)} %get-tuple-element.58) | copy-start | bytes 13828
  640.0 18.1 %copy-start.1 = (bf16[8,120,1152]{2,1,0:T(8,128)(2,1)S(1)}, bf16[8,120,1152]{2,1,0:T(8,128)(2,1)}, u32[]{:S(2)}) copy-start(bf16[8,120,1152]{2,1,0:T(8,128)(2,1)} %param.26) | copy-start | bytes 6635524
Sparse Core Ops, SparseCore 0:
  23.9 55.4 all-gather.2
  263.8 173.0 all-gather.4
where the time goes:
time: 676 us; the launch traced here: 665 us
  matrix products  294 us (43%)
  local copies, waits for them, and re-layouts  160 us (24%)
  waiting for transfers between devices  151 us (22%)
  other arithmetic  45.2 us (7%)
  between operations  14.3 us (2%)
    dot_general x16, matrix products, linear(): jnp.dot(activations, weight, preferred_element_type=jnp.float32)  159 us
    all_gather x2, waiting for transfers between devices, device_fn(): key_vals = lax.all_gather(local_kv, 'sp', axis=1, tiled=True)  151 us
    dot_general x4, matrix products, one_block(): jnp.einsum('bhqk,bkhd->bqhd', attn_probs, value_heads, preferred_element_...  75.2 us
    slice x4, local copies, waits for them, and re-layouts, device_fn(): key_vals[:, :, :model_dim]  65.1 us
    squeeze x4, local copies, waits for them, and re-layouts, attend(): out_blocks = lax.map(one_block, query_blocks)  39.4 us
    sub x1, matrix products, one_block(): attn_probs = jax.nn.softmax(scores, axis=-1).astype(jnp.bfloat16)  37 us
    slice x2, local copies, waits for them, and re-layouts, device_fn(): key_vals[:, :, model_dim:]  31.3 us
    sub x3, other arithmetic, one_block(): attn_probs = jax.nn.softmax(scores, axis=-1).astype(jnp.bfloat16)  22.5 us
  transfers between devices with their start and end apart: 2, of which 2 were waited for; matrix products, arithmetic and copies ran while one was open for 12% of the time, Pallas kernels for 0%

commit v1 on v0

v1 whole, which is shorter than its diff:
```python
import functools, math
import jax, jax.numpy as jnp
from jax import lax
from jax.experimental import pallas as pl
from jax.experimental.pallas import tpu as pltpu
from jax.sharding import PartitionSpec as P

HEAD_DIM = 72
LN_EPS = 1e-6
F32, BF16 = jnp.float32, jnp.bfloat16
SM_SCALE = HEAD_DIM ** -0.5 * math.log2(math.e)
VLIM = 62 * 1024 * 1024


def dotf(a, b):
    return jnp.dot(a, b, preferred_element_type=F32)


def norm(v):
    mean = jnp.mean(v, axis=-1, keepdims=True)
    c = v - mean
    var = jnp.mean(c * c, axis=-1, keepdims=True)
    return c * lax.rsqrt(var + LN_EPS)


def gelu(v):
    k = math.sqrt(2.0 / math.pi)
    t = jnp.tanh(v * (k + (k * 0.044715) * (v * v)))
    hv = 0.5 * v
    return hv + hv * t


def split_heads(ref, val, heads):
    for h in range(heads):
        ref[h] = val[:, h * HEAD_DIM:(h + 1) * HEAD_DIM]


def split_heads_t(ref, val, heads):
    vt = val.T
    for h in range(heads):
        ref[h] = vt[h * HEAD_DIM:(h + 1) * HEAD_DIM, :].astype(BF16)


def attn_head(k, q, vt, bias):
    s = lax.dot_general(k, q, (((1,), (1,)), ((), ())), preferred_element_type=F32)
    if bias is not None:
        s = s + bias
    m = jnp.max(s, axis=0, keepdims=True)
    e = jnp.exp2((s - m) * SM_SCALE)
    l = jnp.sum(e, axis=0, keepdims=True)
    o = dotf(vt, e.astype(BF16))
    return o * (1.0 / l)


def prep0_kernel(x_ref, mods_ref, wq_ref, bq_ref, wkv_ref, bkv_ref, cw_ref, cb_ref, g_ref, b_ref, q_ref, k_ref, v_ref, u_scr, *, layer, width):
    heads = q_ref.shape[0]
    d = x_ref.shape[1]
    u = (norm(x_ref[...].astype(F32)) * (1.0 + mods_ref[1:2, :]) + mods_ref[0:1, :]).astype(BF16)
    q = (dotf(u, wq_ref[...]) + bq_ref[layer:layer + 1, :].astype(F32)).astype(BF16)
    split_heads(q_ref, q, heads)
    uf = u.astype(F32)
    for j in range(d // 128):
        u_scr[j] = uf[:, j * 128:(j + 1) * 128]
    rows = x_ref.shape[0] // width
    parts = []
    for r in range(rows // 2):
        cols = []
        for j in range(d // 128):
            acc = None
            for a in range(2):
                for b in range(2):
                    t = u_scr[j, pl.ds((2 * r + a) * width + b, width // 2, stride=2), :] * cw_ref[a, b:b + 1, j * 128:(j + 1) * 128].astype(F32)
                    acc = t if acc is None else acc + t
            cols.append(acc)
        parts.append(jnp.concatenate(cols, axis=1))
    e = jnp.concatenate(parts, axis=0) + cb_ref[...].astype(F32)
    c = (norm(e) * g_ref[...].astype(F32) + b_ref[...].astype(F32)).astype(BF16)
    kv = dotf(c, wkv_ref[...]) + bkv_ref[layer:layer + 1, :].astype(F32)
    split_heads(k_ref, kv[:, :d].astype(BF16), heads)
    n = kv.shape[0]
    for h in range(heads):
        pass
    vt = kv[:, d:].T
    for h in range(heads):
        v_ref[h] = vt[h * HEAD_DIM:(h + 1) * HEAD_DIM, :].astype(BF16)


def prep1_kernel(x_ref, mods_ref, wq_ref, bq_ref, wkv_ref, bkv_ref, q_ref, k_ref, v_ref, *, layer):
    heads = q_ref.shape[0]
    d = x_ref.shape[1]
    u = (norm(x_ref[...].astype(F32)) * (1.0 + mods_ref[1:2, :]) + mods_ref[0:1, :]).astype(BF16)
    q = (dotf(u, wq_ref[...]) + bq_ref[layer:layer + 1, :].astype(F32)).astype(BF16)
    split_heads(q_ref, q, heads)
    kv = dotf(u, wkv_ref[...]) + bkv_ref[layer:layer + 1, :].astype(F32)
    split_heads(k_ref, kv[:, :d].astype(BF16), heads)
    split_heads_t(v_ref, kv[:, d:], heads)


def full(shape):
    n = len(shape)
    return pl.BlockSpec(shape, lambda *_: (0,) * n, pipeline_mode=pl.Buffered(1))


def layered(shape, layer):
    n = len(shape) - 1
    return pl.BlockSpec((None,) + tuple(shape[1:]), lambda *_: (layer,) + (0,) * n, pipeline_mode=pl.Buffered(1))


def prep(layer, x, mods, wq, bq, wkv, bkv, comp, width):
    t, d = x.shape
    heads = d // HEAD_DIM
    tm = 256
    ins = [x, mods, wq, bq, wkv, bkv]
    specs = [pl.BlockSpec((tm, d), lambda r: (r, 0)), layered(mods.shape, layer), layered(wq.shape, layer), full(bq.shape), layered(wkv.shape, layer), full(bkv.shape)]
    if comp is not None:
        ins += list(comp)
        specs += [full(a.shape) for a in comp]
        nk, kern, scr = tm // 4, functools.partial(prep0_kernel, layer=layer, width=width), [pltpu.VMEM((d // 128, tm, 128), F32)]
    else:
        nk, kern, scr = tm, functools.partial(prep1_kernel, layer=layer), []
    s = t * nk // tm
    if comp is None:
        vshape, vspec = (heads, HEAD_DIM, s), pl.BlockSpec((heads, HEAD_DIM, nk), lambda r: (0, 0, r))
    else:
        vshape, vspec = (t // tm, heads, HEAD_DIM, nk), pl.BlockSpec((None, heads, HEAD_DIM, nk), lambda r: (r, 0, 0, 0))
    q, k, v = pl.pallas_call(
        kern, grid=(t // tm,), in_specs=specs,
        out_specs=[pl.BlockSpec((heads, tm, HEAD_DIM), lambda r: (0, r, 0)), pl.BlockSpec((heads, nk, HEAD_DIM), lambda r: (0, r, 0)), vspec],
        out_shape=[jax.ShapeDtypeStruct((heads, t, HEAD_DIM), BF16), jax.ShapeDtypeStruct((heads, s, HEAD_DIM), BF16), jax.ShapeDtypeStruct(vshape, BF16)],
        scratch_shapes=scr,
        compiler_params=pltpu.CompilerParams(vmem_limit_bytes=VLIM),
        name=f"prep{layer}",
    )(*ins)
    if comp is not None:
        v = jnp.moveaxis(v, 0, 2).reshape(heads, HEAD_DIM, s)
    return q, k, v


def cap_kernel(cap_ref, w_ref, b_ref, k_ref, v_ref, c_scr):
    heads, n, _ = k_ref.shape
    d = cap_ref.shape[1]
    c_scr[...] = jnp.zeros_like(c_scr)
    c_scr[:cap_ref.shape[0], :] = cap_ref[...]
    kv = dotf(c_scr[...], w_ref[...]) + b_ref[...].astype(F32)
    split_heads(k_ref, kv[:, :d].astype(BF16), heads)
    split_heads_t(v_ref, kv[:, d:], heads)


def cap_kv(cap, w, b):
    n, d = cap.shape
    layers = w.shape[0]
    heads = d // HEAD_DIM
    npad = -(-n // 128) * 128
    return pl.pallas_call(
        cap_kernel, grid=(layers,),
        in_specs=[full(cap.shape), pl.BlockSpec((None,) + w.shape[1:], lambda l: (l, 0, 0)), pl.BlockSpec((None, 1, w.shape[2]), lambda l: (l, 0, 0))],
        out_specs=[pl.BlockSpec((None, heads, npad, HEAD_DIM), lambda l: (l, 0, 0, 0)), pl.BlockSpec((None, heads, HEAD_DIM, npad), lambda l: (l, 0, 0, 0))],
        out_shape=[jax.ShapeDtypeStruct((layers, heads, npad, HEAD_DIM), BF16), jax.ShapeDtypeStruct((layers, heads, HEAD_DIM, npad), BF16)],
        scratch_shapes=[pltpu.VMEM((npad, d), BF16)],
        compiler_params=pltpu.CompilerParams(vmem_limit_bytes=VLIM),
        name="capkv",
    )(cap, w, b[:, None, :])


UNROLL = 2


def tail_kernel(x_ref, q_ref, k_ref, v_ref, kc_ref, vc_ref, cb_ref, mods_ref, wo_ref, bo_ref, cwq_ref, cbq_ref, cwo_ref, cbo_ref, w1_ref, b1_ref, w2_ref, b2_ref,
                o_ref, ot_scr, qc_scr, h_scr, *, layer):
    heads = q_ref.shape[0]
    d = x_ref.shape[1]
    f = w1_ref.shape[1]
    row = lambda r: r[layer:layer + 1, :].astype(F32)

    def self_body(h, _):
        ot_scr[h] = attn_head(k_ref[h], q_ref[h], v_ref[h], None)
        return 0

    lax.fori_loop(0, heads, self_body, 0, unroll=UNROLL)
    o = ot_scr[...].reshape(d, -1).T.astype(BF16)
    x = x_ref[...].astype(F32)
    x = (x + mods_ref[2:3, :] * (dotf(o, wo_ref[...]) + row(bo_ref))).astype(BF16)
    qc = (dotf(x, cwq_ref[...]) + row(cbq_ref)).astype(BF16)
    split_heads(qc_scr, qc, heads)
    cbias = cb_ref[...]

    def cross_body(h, _):
        ot_scr[h] = attn_head(kc_ref[h], qc_scr[h], vc_ref[h], cbias)
        return 0

    lax.fori_loop(0, heads, cross_body, 0, unroll=UNROLL)
    o = ot_scr[...].reshape(d, -1).T.astype(BF16)
    x = (x.astype(F32) + (dotf(o, cwo_ref[...]) + row(cbo_ref))).astype(BF16)
    u = (norm(x.astype(F32)) * (1.0 + mods_ref[4:5, :]) + mods_ref[3:4, :]).astype(BF16)
    fb = 512
    for j in range(f // fb):
        sl = slice(j * fb, (j + 1) * fb)
        h_scr[:, sl] = gelu(dotf(u, w1_ref[:, sl]) + b1_ref[layer:layer + 1, sl].astype(F32)).astype(BF16)
    y = dotf(h_scr[...], w2_ref[...]) + row(b2_ref)
    o_ref[...] = (x.astype(F32) + mods_ref[5:6, :] * y).astype(BF16)


def tail(layer, x, q, k, v, kc, vc, cbias, mods, wo, bo, cwq, cbq, cwo, cbo, w1, b1, w2, b2):
    t, d = x.shape
    heads = d // HEAD_DIM
    tm = 256
    L = functools.partial(lambda a: layered(a.shape, layer))
    Fu = lambda a: full(a.shape)
    rowspec = pl.BlockSpec((tm, d), lambda r: (r, 0))
    return pl.pallas_call(
        functools.partial(tail_kernel, layer=layer), grid=(t // tm,),
        in_specs=[rowspec, pl.BlockSpec((heads, tm, HEAD_DIM), lambda r: (0, r, 0)), Fu(k), Fu(v), L(kc), L(vc), Fu(cbias), L(mods), L(wo), Fu(bo), L(cwq), Fu(cbq), L(cwo), Fu(cbo), L(w1), Fu(b1), L(w2), Fu(b2)],
        out_specs=rowspec, out_shape=jax.ShapeDtypeStruct((t, d), BF16),
        scratch_shapes=[pltpu.VMEM((heads, HEAD_DIM, tm), F32), pltpu.VMEM((heads, tm, HEAD_DIM), BF16), pltpu.VMEM((tm, w1.shape[2]), BF16)],
        compiler_params=pltpu.CompilerParams(vmem_limit_bytes=VLIM),
        name=f"tail{layer}",
    )(x, q, k, v, kc, vc, cbias, mods, wo, bo, cwq, cbq, cwo, cbo, w1, b1, w2, b2)


def image_core(x, cap, valid, te, width, ada_table, attn_wq, attn_bq, attn_wkv, attn_bkv, attn_wo, attn_bo, comp_w, comp_b, cnorm_g, cnorm_b, cross_wq, cross_bq, cross_wkv, cross_bkv, cross_wo, cross_bo, mlp_w1, mlp_b1, mlp_w2, mlp_b2):
    d = x.shape[1]
    n = cap.shape[0]
    npad = -(-n // 128) * 128
    mods = te.astype(F32).reshape(6, d)[None] + ada_table.astype(F32)
    cbias = jnp.where(valid > 0, 0.0, -1e9).astype(F32) / HEAD_DIM ** -0.5
    cbias = jnp.pad(cbias, (0, npad - n), constant_values=-jnp.inf)[:, None]
    kc, vc = cap_kv(cap, cross_wkv, cross_bkv)
    comp = (comp_w, comp_b[None], cnorm_g[None], cnorm_b[None])
    for layer in range(2):
        q, k, v = prep(layer, x, mods, attn_wq, attn_bq, attn_wkv, attn_bkv, comp if layer == 0 else None, width)
        x = tail(layer, x, q, k, v, kc, vc, cbias, mods, attn_wo, attn_bo, cross_wq, cross_bq, cross_wo, cross_bo, mlp_w1, mlp_b1, mlp_w2, mlp_b2)
    return x


def exchange_kernel(x_ref, o_ref, send_sem, recv_sem, *, axis):
    n = x_ref.shape[0]
    me = lax.axis_index(axis)
    barrier = pltpu.get_barrier_semaphore()
    for k in range(1, n):
        pl.semaphore_signal(barrier, inc=1, device_id={axis: lax.rem(me + k, n)}, device_id_type=pl.DeviceIdType.MESH)
    pl.semaphore_wait(barrier, n - 1)
    copies = []
    for k in range(1, n):
        peer = lax.rem(me + k, n)
        cp = pltpu.make_async_remote_copy(src_ref=x_ref.at[peer], dst_ref=o_ref.at[me], send_sem=send_sem.at[k - 1], recv_sem=recv_sem.at[k - 1],
                                          device_id={axis: peer}, device_id_type=pl.DeviceIdType.MESH)
        cp.start()
        copies.append(cp)
    o_ref[me] = x_ref[me]
    for cp in copies:
        cp.wait()


def exchange(x, axis, cid):
    n = x.shape[0]
    return pl.pallas_call(
        functools.partial(exchange_kernel, axis=axis),
        in_specs=[pl.BlockSpec(memory_space=pltpu.VMEM)], out_specs=pl.BlockSpec(memory_space=pltpu.VMEM),
        out_shape=jax.ShapeDtypeStruct(x.shape, x.dtype),
        scratch_shapes=[pltpu.SemaphoreType.DMA((n - 1,)), pltpu.SemaphoreType.DMA((n - 1,))],
        compiler_params=pltpu.CompilerParams(collective_id=cid, has_side_effects=True, vmem_limit_bytes=VLIM),
        name=f"exchange{cid}",
    )(x)


def solution(mesh):
    in_specs = (P('dp', 'sp', None, None), P('dp', None, None), P('dp', None), P('dp', None)) + (P(),) * 21
    out_specs = P('dp', 'sp', None, None)
    n = mesh.shape['sp']

    def device_fn(tokens, caption, cap_valid, time_emb, *weights):
        b, rows, width, d = tokens.shape
        assert b == n
        img = lax.axis_index('sp')
        pick = lambda a: lax.dynamic_index_in_dim(a, img, 0, keepdims=False)
        x = exchange(tokens.reshape(b, rows * width, d), 'sp', 0)
        y = image_core(x.reshape(b * rows * width, d), pick(caption), pick(cap_valid), pick(time_emb), width, *weights)
        return exchange(y.reshape(b, rows * width, d), 'sp', 1).reshape(tokens.shape)

    return jax.shard_map(device_fn, mesh=mesh, in_specs=in_specs, out_specs=out_specs, check_vma=False)
```

time: 676 us -> 334 us (0.49); the launches traced: 665 us -> 333 us
  Pallas kernels: 0 us -> 315 us
  matrix products: 294 us -> 0 us
  waiting for transfers between devices: 151 us -> 0 us
  local copies, waits for them, and re-layouts: 160 us -> 14.6 us
  other arithmetic: 45.2 us -> 3.06 us
  between operations: 14.3 us -> 0.04 us
    pallas_call x0 -> x7, Pallas kernels: none -> 315 us  [the longest x2 210 us: tail(): pl.pallas_call(functools.partial(tail_kernel, layer=layer), grid=(t // tm...]
    dot_general x23 -> x0, matrix products: 257 us -> none  [the longest x16 159 us: linear(): jnp.dot(activations, weight, preferred_element_type=jnp.float32)]
    all_gather x2 -> x0, waiting for transfers between devices: 151 us -> none  [device_fn(): key_vals = lax.all_gather(local_kv, 'sp', axis=1, tiled=True)]
    slice x13 -> x0, local copies, waits for them, and re-layouts: 117 us -> none  [the longest x4 65.1 us: device_fn(): key_vals[:, :, :model_dim]]
    squeeze x4 -> x1, local copies, waits for them, and re-layouts: 39.4 us -> 1.68 us  [device_fn(): pick = lambda a: lax.dynamic_index_in_dim(a, img, 0, keepdims=False)]
    sub x1 -> x0, matrix products: 37 us -> none  [one_block(): attn_probs = jax.nn.softmax(scores, axis=-1).astype(jnp.bfloat16)]
    sub x3 -> x0, other arithmetic: 22.5 us -> none  [one_block(): attn_probs = jax.nn.softmax(scores, axis=-1).astype(jnp.bfloat16)]
    reduce_sum x11 -> x0, other arithmetic: 12.9 us -> none  [the longest x2 5.97 us: compress(): jnp.sum(grid_view * conv_w.astype(jnp.float32)[:, None, :, :], axis=(2, 4))]
  transfers between devices with their start and end apart: 2 -> 0, of which waited for: 2 -> 0; matrix products, arithmetic and copies ran while one was open for 12% -> 0% of each run, Pallas kernels for 0% -> 0%
where the time goes in v1:
time: 334 us; the launch traced here: 333 us
  Pallas kernels  315 us (94%)
  local copies, waits for them, and re-layouts  14.6 us (4%)
    pallas_call x2, Pallas kernels, tail(): pl.pallas_call(functools.partial(tail_kernel, layer=layer), grid=(t // tm...  210 us
    pallas_call x2, Pallas kernels, exchange(): pl.pallas_call(functools.partial(exchange_kernel, axis=axis), in_specs=[p...  67.7 us
    pallas_call x2, Pallas kernels, prep(): pl.pallas_call(kern, grid=(t // tm,), in_specs=specs, out_specs=[pl.Block...  31.4 us

profile of v1, /device:TPU:81, one launch (start us, length us, event | category | flops | bytes accessed | tf_op | source)
XLA Modules:
  0.0 333.1 jit_solution(11817030391428270464)
XLA Ops:
  0.0 0.7 multiply_bitcast_fusion
  0.7 1.3 broadcast_in_dim.23.cb_ref
  2.0 1.3 broadcast_in_dim.24.g_ref
  3.3 1.3 broadcast_in_dim.25.b_ref
  4.5 1.3 copy.32.b_ref
  5.8 1.0 convert_reduce_fusion
  6.8 1.4 convert_add_fusion.mods_ref
  8.2 0.7 copy.33.cb_ref
  9.0 1.7 dynamic-slice_bitcast_fusion.cap_ref
  10.6 5.9 %capkv.1 = (bf16[2,16,128,72]{3,2,1,0:T(8,128)(2,1)}, bf16[2,16,72,128]{3,2,1,0:T(8,128)(2,1)}) custom-call(bf16[120,1152]{1,0:T(8,128)(2,1)} %dynamic-slice_bitcast_fusion.cap_ref, bf16[2,1152,2304]{2,1,0:T(8,128)(2,1)} %w_ref.1, bf16[2,1,2304]{2,1,0:T(2,128)(2,1)} %copy.32.b_ref), custom_call_target="tpu_custom_call" | custom-call | tf_op jit(solution)/shard_map/capkv/pallas_call | solution.py:154
  16.6 35.1 %exchange0.1 = bf16[8,128,1152]{2,1,0:T(8,128)(2,1)} custom-call(bf16[8,128,1152]{2,1,0:T(8,128)(2,1)} %bitcast.16), custom_call_target="tpu_custom_call" | custom-call | tf_op jit(solution)/shard_map/exchange0/pallas_call | solution.py:256
  51.7 14.4 %prep0.1 = (bf16[16,1024,72]{2,1,0:T(8,128)(2,1)}, bf16[16,256,72]{2,1,0:T(8,128)(2,1)}, bf16[4,16,72,64]{3,2,1,0:T(8,128)(2,1)}) custom-call(bf16[1024,1152]{1,0:T(8,128)(2,1)} %bitcast.12, f32[2,6,1152]{2,1,0:T(8,128)} %convert_add_fusion.mods_ref, bf16[2,1152,1152]{2,1,0:T(8,128)(2,1)} %wq_ref.3, bf16[2,1152]{1,0:T(2,128)(2,1)} %bq_ref.3, ...), custom_call_target="tpu_custom_call" | custom-call | tf_op jit(solution)/shard_map/prep0/pallas_call | solution.py:126
  66.1 2.2 copy.31
  68.3 1.6 reshape.31.v_ref
  69.9 92.7 %tail0.1.x_ref = bf16[1024,1152]{1,0:T(8,128)(2,1)} custom-call(bf16[1024,1152]{1,0:T(8,128)(2,1)} %bitcast.13, bf16[16,1024,72]{2,1,0:T(8,128)(2,1)} %get-tuple-element.13.q_ref, bf16[16,256,72]{2,1,0:T(8,128)(2,1)} %get-tuple-element.14.k_ref, bf16[16,72,256]{2,1,0:T(8,128)(2,1)} %reshape.31.v_ref, bf16[2,16,128,72]{3,2,1,0:T(8,128)(2,1)} %get-tuple-element.16.kc_ref, ...), custom_call_target="tpu_custom_call" | custom-call | tf_op jit(solution)/shard_map/tail0/pallas_call | solution.py:210
  162.6 16.9 %prep1.1 = (bf16[16,1024,72]{2,1,0:T(8,128)(2,1)}, bf16[16,1024,72]{2,1,0:T(8,128)(2,1)}, bf16[16,72,1024]{2,1,0:T(8,128)(2,1)}) custom-call(bf16[1024,1152]{1,0:T(8,128)(2,1)} %tail0.1.x_ref, f32[2,6,1152]{2,1,0:T(8,128)} %convert_add_fusion.mods_ref, bf16[2,1152,1152]{2,1,0:T(8,128)(2,1)} %wq_ref.3, bf16[2,1152]{1,0:T(2,128)(2,1)} %bq_ref.3, ...), custom_call_target="tpu_custom_call" | custom-call | tf_op jit(solution)/shard_map/prep1/pallas_call | solution.py:126
  179.5 117.7 %tail1.1 = bf16[1024,1152]{1,0:T(8,128)(2,1)} custom-call(bf16[1024,1152]{1,0:T(8,128)(2,1)} %tail0.1.x_ref, bf16[16,1024,72]{2,1,0:T(8,128)(2,1)} %get-tuple-element.18.q_ref, bf16[16,1024,72]{2,1,0:T(8,128)(2,1)} %get-tuple-element.19.k_ref, bf16[16,72,1024]{2,1,0:T(8,128)(2,1)} %get-tuple-element.20.v_ref, ...), custom_call_target="tpu_custom_call" | custom-call | tf_op jit(solution)/shard_map/tail1/pallas_call | solution.py:210
  297.2 32.6 %exchange1.1 = bf16[8,128,1152]{2,1,0:T(8,128)(2,1)} custom-call(bf16[8,128,1152]{2,1,0:T(8,128)(2,1)} %bitcast.14), custom_call_target="tpu_custom_call" | custom-call | tf_op jit(solution)/shard_map/exchange1/pallas_call | solution.py:256
  329.8 3.3 copy.37
  (2 shorter events, 0.0 us)

commit v2 on v0

v2 whole, which is shorter than its diff:
```python
import functools, math
import jax
import jax.numpy as jnp
from jax import lax
from jax.experimental import pallas as pl
from jax.experimental.pallas import tpu as pltpu
from jax.sharding import PartitionSpec as P

HEAD_DIM = 72
LN_EPS = 1e-6
F32, BF16 = jnp.float32, jnp.bfloat16
SM_SCALE = HEAD_DIM ** -0.5 * math.log2(math.e)
VLIM = 66_900_000
CH = 256
WEIGHTS = ('wq', 'wkv', 'wo', 'cwq', 'cwo', 'w1', 'w2')
SLABS = 4


def dotf(a, b):
    return jnp.dot(a, b, preferred_element_type=F32)


def norm(v):
    mean = jnp.mean(v, axis=-1, keepdims=True)
    c = v - mean
    var = jnp.mean(c * c, axis=-1, keepdims=True)
    return c * lax.rsqrt(var + LN_EPS)


def gelu(v):
    k = math.sqrt(2.0 / math.pi)
    t = jnp.tanh(v * (k + (k * 0.044715) * (v * v)))
    hv = 0.5 * v
    return hv + hv * t


def fold(v, op):
    return op(v.reshape(v.shape[0] // 8, 8, v.shape[1]), axis=0)


def attention(q_at, k_at, v_at, ot_ref, sa, sb, nb, kb_size, heads, bias_at, unroll):
    def scores(h, kb, q):
        s = lax.dot_general(k_at(h, kb), q, (((1,), (1,)), ((), ())), preferred_element_type=F32)
        return s if bias_at is None else s + bias_at(kb)

    def first():
        q = q_at(0)
        mx = None
        for kb in range(nb):
            s = scores(0, kb, q)
            sa[kb * kb_size:(kb + 1) * kb_size, :] = s
            f = fold(s, jnp.max)
            mx = f if mx is None else jnp.maximum(mx, f)
        return mx

    def step(h, hn, mx, cur, nxt):
        m = jnp.max(mx, axis=0, keepdims=True)
        q = q_at(hn)
        mn = l = acc = None
        for kb in range(nb):
            sl = slice(kb * kb_size, (kb + 1) * kb_size)
            s = scores(hn, kb, q)
            nxt[sl, :] = s
            f = fold(s, jnp.max)
            mn = f if mn is None else jnp.maximum(mn, f)
            e = jnp.exp2((cur[sl, :] - m) * SM_SCALE)
            f = fold(e, jnp.sum)
            l = f if l is None else l + f
            a = dotf(v_at(h, kb), e.astype(BF16))
            acc = a if acc is None else acc + a
        l = jnp.sum(l, axis=0, keepdims=True)
        ot_ref[h] = acc * (1.0 / l)
        return mn

    def body(i, mx):
        h = 2 * i
        mx = step(h, h + 1, mx, sa, sb)
        return step(h + 1, jnp.minimum(h + 2, heads - 1), mx, sb, sa)

    lax.fori_loop(0, heads // 2, body, first(), unroll=unroll)


def mega_kernel(*refs, axis, width):
    (x_hbm, cap_hbm, valid_ref, te_ref, tab_ref, bq_ref, bkv_ref, bo_ref, cw_ref, cb_ref, g_ref, gb_ref, cbq_ref, cbkv_ref, cbo_ref, b1_ref, b2_ref,
     wq_hbm, wkv_hbm, wo_hbm, cwq_hbm, cwkv_hbm, cwo_hbm, w1_hbm, w2_hbm, out_hbm,
     wq, wkv, wo, cwq, cwo, w1, w2, x_scr, q_scr, k_scr, vt_scr, kc_scr, vc_scr, cap_scr, vb_scr, bias_scr, mods, sa, sb, sc, sd, ot, h_scr, u_scr, c_scr,
     wsem, csem, xsem, capsem, osem) = refs
    t, d = x_scr.shape
    heads = q_scr.shape[0]
    f = w1.shape[1]
    nkeys0 = t // 4
    ncap = kc_scr.shape[2]
    img = lax.axis_index(axis)
    hbm = dict(zip(WEIGHTS, (wq_hbm, wkv_hbm, wo_hbm, cwq_hbm, cwo_hbm, w1_hbm, w2_hbm)))
    buf = dict(zip(WEIGHTS, (wq, wkv, wo, cwq, cwo, w1, w2)))

    def wcopies(name, layer):
        i = WEIGHTS.index(name)
        rows = buf[name].shape[0] // SLABS
        return [pltpu.make_async_copy(hbm[name].at[layer, pl.ds(s * rows, rows)], buf[name].at[pl.ds(s * rows, rows)], wsem.at[i, s]) for s in range(SLABS)]

    def wstart(name, layer):
        for c in wcopies(name, layer):
            c.start()

    def wwait(name, layer):
        for c in wcopies(name, layer):
            c.wait()

    capcopy = pltpu.make_async_copy(cap_hbm.at[img], cap_scr.at[pl.ds(0, cap_hbm.shape[1])], capsem)
    ccopies = [pltpu.make_async_copy(cwkv_hbm.at[l], w1.at[:, pl.ds(l * 2 * d, 2 * d)], csem.at[l]) for l in range(2)]
    xcopies = [pltpu.make_async_copy(x_hbm.at[pl.ds(c * CH, CH)], x_scr.at[pl.ds(c * CH, CH)], xsem.at[c]) for c in range(t // CH)]
    cap_scr[cap_hbm.shape[1]:, :] = jnp.zeros((ncap - cap_hbm.shape[1], d), BF16)
    capcopy.start()
    for c in ccopies:
        c.start()
    for c in xcopies:
        c.start()
    for name in ('wq', 'wkv', 'wo', 'cwq', 'cwo', 'w2'):
        wstart(name, 0)

    pick = lax.broadcasted_iota(jnp.int32, (te_ref.shape[0], 1), 0) == img
    te = jnp.sum(jnp.where(pick, te_ref[...].astype(F32), 0.0), axis=0, keepdims=True)
    for l in range(2):
        for j in range(6):
            mods[l, j:j + 1, :] = te[:, j * d:(j + 1) * d] + tab_ref[l, j:j + 1, :].astype(F32)
    vb_scr[...] = jnp.full(vb_scr.shape, -jnp.inf, F32)
    valid = jnp.sum(jnp.where(pick, valid_ref[...], 0), axis=0, keepdims=True)
    vb = jnp.where(valid > 0, 0.0, -1e9 / HEAD_DIM ** -0.5).astype(F32)
    vb_scr[:, :valid.shape[1]] = jnp.broadcast_to(vb, (8, valid.shape[1]))
    bias_scr[...] = vb_scr[...].T[:, 0:1]

    def store_heads(ref, rows, val):
        for h in range(heads):
            ref[h, rows, :] = val[:, h * HEAD_DIM:(h + 1) * HEAD_DIM]

    def store_heads_t(ref, cols, val):
        vt = val.T
        for h in range(heads):
            ref[h, :, cols] = vt[h * HEAD_DIM:(h + 1) * HEAD_DIM, :].astype(BF16)

    def row(ref, layer):
        return ref[layer:layer + 1, :].astype(F32)

    def modulate(v, layer, j):
        return (norm(v) * (1.0 + mods[layer, j + 1:j + 2, :]) + mods[layer, j:j + 1, :]).astype(BF16)

    capcopy.wait()
    for l in range(2):
        ccopies[l].wait()
        for part in range(2):
            lo = l * 2 * d + part * d
            y = dotf(cap_scr[...], w1[:, lo:lo + d]) + cbkv_ref[l:l + 1, part * d:(part + 1) * d].astype(F32)
            if part == 0:
                store_heads(kc_scr.at[l], slice(None), y.astype(BF16))
            else:
                store_heads_t(vc_scr.at[l], slice(None), y)
    wstart('w1', 0)

    wwait('wq', 0)
    for c in xcopies:
        c.wait()

    def prep0(c, _):
        rows = pl.ds(pl.multiple_of(c * CH, CH), CH)
        u = modulate(x_scr[rows, :].astype(F32), 0, 0)
        store_heads(q_scr, rows, (dotf(u, wq[...]) + row(bq_ref, 0)).astype(BF16))
        uf = u.astype(F32)
        for j in range(d // 128):
            u_scr[j] = uf[:, j * 128:(j + 1) * 128]
        parts = []
        for r in range(CH // width // 2):
            cols = []
            for j in range(d // 128):
                acc = None
                for a in range(2):
                    for b in range(2):
                        w = cw_ref[a, b:b + 1, j * 128:(j + 1) * 128].astype(F32)
                        v = u_scr[j, pl.ds((2 * r + a) * width + b, width // 2, stride=2), :] * w
                        acc = v if acc is None else acc + v
                cols.append(acc)
            parts.append(jnp.concatenate(cols, axis=1))
        e = jnp.concatenate(parts, axis=0) + cb_ref[...].reshape(1, d).astype(F32)
        y = norm(e) * g_ref[...].reshape(1, d).astype(F32) + gb_ref[...].reshape(1, d).astype(F32)
        c_scr[pl.ds(pl.multiple_of(c * (CH // 4), CH // 4), CH // 4), :] = y.astype(BF16)
        return 0

    lax.fori_loop(0, t // CH, prep0, 0)
    wstart('wq', 1)
    wwait('wkv', 0)
    store_heads(k_scr, slice(0, nkeys0), (dotf(c_scr[...], wkv[:, :d]) + bkv_ref[0:1, :d].astype(F32)).astype(BF16))
    store_heads_t(vt_scr, slice(0, nkeys0), dotf(c_scr[...], wkv[:, d:]) + bkv_ref[0:1, d:].astype(F32))
    wstart('wkv', 1)

    def tail(layer, tq, nkeys, sx, sy, unroll):
        last = t // tq - 1
        kb = min(nkeys, 256)
        halves = tq // CH

        def chunk(c, _):
            base = pl.multiple_of(c * tq, tq)
            rows = pl.ds(base, tq)
            half = [pl.ds(pl.multiple_of(base + i * CH, CH), CH) for i in range(halves)]

            def first_use(name):
                @pl.when(c == 0)
                def _():
                    wwait(name, layer)

            def last_use(name):
                if layer == 0:
                    @pl.when(c == last)
                    def _():
                        wstart(name, 1)

            attention(lambda h: q_scr[h, rows, :], lambda h, i: k_scr[h, i * kb:(i + 1) * kb, :], lambda h, i: vt_scr[h, :, i * kb:(i + 1) * kb],
                      ot.at[:, :, :tq], sx, sy, nkeys // kb, kb, heads, None, unroll)
            first_use('wo')
            first_use('cwq')
            for i in range(halves):
                o = ot[:, :, i * CH:(i + 1) * CH].reshape(d, CH).T.astype(BF16)
                x = x_scr[half[i], :].astype(F32)
                x = (x + mods[layer, 2:3, :] * (dotf(o, wo[...]) + row(bo_ref, layer))).astype(BF16)
                x_scr[half[i], :] = x
                store_heads(q_scr, half[i], (dotf(x, cwq[...]) + row(cbq_ref, layer)).astype(BF16))
            last_use('wo')
            last_use('cwq')
            attention(lambda h: q_scr[h, rows, :], lambda h, i: kc_scr[layer, h], lambda h, i: vc_scr[layer, h],
                      ot.at[:, :, :tq], sc.at[:, :tq], sd.at[:, :tq], 1, ncap, heads, lambda i: bias_scr[...], 8)
            first_use('cwo')
            for i in range(halves):
                o = ot[:, :, i * CH:(i + 1) * CH].reshape(d, CH).T.astype(BF16)
                x_scr[half[i], :] = (x_scr[half[i], :].astype(F32) + (dotf(o, cwo[...]) + row(cbo_ref, layer))).astype(BF16)
            last_use('cwo')
            first_use('w1')
            first_use('w2')

            def mlp(i, _):
                r = pl.ds(pl.multiple_of(base + i * CH, CH), CH)
                u = modulate(x_scr[r, :].astype(F32), layer, 3)
                fb = 512
                for j in range(f // fb):
                    sl = slice(j * fb, (j + 1) * fb)
                    h_scr[:, sl] = gelu(dotf(u, w1[:, sl]) + b1_ref[layer:layer + 1, sl].astype(F32)).astype(BF16)
                y = dotf(h_scr[...], w2[...]) + row(b2_ref, layer)
                x_scr[r, :] = (x_scr[r, :].astype(F32) + mods[layer, 5:6, :] * y).astype(BF16)
                return 0

            if halves == 1:
                mlp(0, 0)
            else:
                lax.fori_loop(0, halves, mlp, 0)
            last_use('w1')
            last_use('w2')
            if layer == 1:
                for i in range(halves):
                    pltpu.make_async_copy(x_scr.at[half[i]], out_hbm.at[half[i]], osem).start()
            return 0

        lax.fori_loop(0, t // tq, chunk, 0)

    tail(0, 2 * CH, nkeys0, sc, sd, 4)

    wwait('wq', 1)
    wwait('wkv', 1)

    def prep1(c, _):
        rows = pl.ds(pl.multiple_of(c * CH, CH), CH)
        u = modulate(x_scr[rows, :].astype(F32), 1, 0)
        store_heads(q_scr, rows, (dotf(u, wq[...]) + row(bq_ref, 1)).astype(BF16))
        store_heads(k_scr, rows, (dotf(u, wkv[:, :d]) + bkv_ref[1:2, :d].astype(F32)).astype(BF16))
        store_heads_t(vt_scr, rows, dotf(u, wkv[:, d:]) + bkv_ref[1:2, d:].astype(F32))
        return 0

    lax.fori_loop(0, t // CH, prep1, 0)
    tail(1, CH, t, sa, sb, 2)
    pltpu.make_async_copy(x_scr, out_hbm, osem).wait()


def image_core(x, caption, cap_valid, time_emb, axis, width, ada_table, attn_wq, attn_bq, attn_wkv, attn_bkv, attn_wo, attn_bo, comp_w, comp_b, cnorm_g, cnorm_b, cross_wq, cross_bq, cross_wkv, cross_bkv, cross_wo, cross_bo, mlp_w1, mlp_b1, mlp_w2, mlp_b2):
    t, d = x.shape
    f = mlp_w1.shape[2]
    heads = d // HEAD_DIM
    ncap = -(-caption.shape[1] // 128) * 128
    vmem = [cap_valid, time_emb, ada_table, attn_bq, attn_bkv, attn_bo, comp_w, comp_b, cnorm_g, cnorm_b, cross_bq, cross_bkv, cross_bo, mlp_b1, mlp_b2]
    weights = [attn_wq, attn_wkv, attn_wo, cross_wq, cross_wkv, cross_wo, mlp_w1, mlp_w2]
    anyspec = pl.BlockSpec(memory_space=pl.ANY)
    V = pltpu.VMEM
    scratch = [V((d, d), BF16), V((d, 2 * d), BF16), V((d, d), BF16), V((d, d), BF16), V((d, d), BF16), V((d, f), BF16), V((f, d), BF16),
               V((t, d), BF16), V((heads, t, HEAD_DIM), BF16), V((heads, t, HEAD_DIM), BF16), V((heads, HEAD_DIM, t), BF16),
               V((2, heads, ncap, HEAD_DIM), BF16), V((2, heads, HEAD_DIM, ncap), BF16), V((ncap, d), BF16), V((8, ncap), F32), V((ncap, 1), F32), V((2, 6, d), F32),
               V((t, CH), F32), V((t, CH), F32), V((t // 4, 2 * CH), F32), V((t // 4, 2 * CH), F32), V((heads, HEAD_DIM, 2 * CH), F32), V((CH, f), BF16),
               V((d // 128, CH, 128), F32), V((t // 4, d), BF16),
               pltpu.SemaphoreType.DMA((len(WEIGHTS), SLABS)), pltpu.SemaphoreType.DMA((2,)), pltpu.SemaphoreType.DMA((t // CH,)), pltpu.SemaphoreType.DMA, pltpu.SemaphoreType.DMA]
    return pl.pallas_call(
        functools.partial(mega_kernel, axis=axis, width=width),
        in_specs=[anyspec, anyspec] + [pl.BlockSpec(memory_space=V)] * len(vmem) + [anyspec] * len(weights),
        out_specs=anyspec, out_shape=jax.ShapeDtypeStruct((t, d), BF16), scratch_shapes=scratch,
        compiler_params=pltpu.CompilerParams(vmem_limit_bytes=VLIM),
        name="blocks",
    )(x, caption, *vmem, *weights)


def exchange_kernel(x_ref, o_ref, send_sem, recv_sem, *, axis):
    n = x_ref.shape[0]
    me = lax.axis_index(axis)
    barrier = pltpu.get_barrier_semaphore()
    for k in range(1, n):
        pl.semaphore_signal(barrier, inc=1, device_id={axis: lax.rem(me + k, n)}, device_id_type=pl.DeviceIdType.MESH)
    pl.semaphore_wait(barrier, n - 1)
    copies = []
    for k in range(1, n):
        peer = lax.rem(me + k, n)
        cp = pltpu.make_async_remote_copy(src_ref=x_ref.at[peer], dst_ref=o_ref.at[me], send_sem=send_sem.at[k - 1], recv_sem=recv_sem.at[k - 1],
                                          device_id={axis: peer}, device_id_type=pl.DeviceIdType.MESH)
        cp.start()
        copies.append(cp)
    o_ref[me] = x_ref[me]
    for cp in copies:
        cp.wait()


def exchange(x, axis, cid):
    n = x.shape[0]
    return pl.pallas_call(
        functools.partial(exchange_kernel, axis=axis),
        in_specs=[pl.BlockSpec(memory_space=pltpu.VMEM)], out_specs=pl.BlockSpec(memory_space=pltpu.VMEM),
        out_shape=jax.ShapeDtypeStruct(x.shape, x.dtype),
        scratch_shapes=[pltpu.SemaphoreType.DMA((n - 1,)), pltpu.SemaphoreType.DMA((n - 1,))],
        compiler_params=pltpu.CompilerParams(collective_id=cid, has_side_effects=True, vmem_limit_bytes=VLIM),
        name=f"exchange{cid}",
    )(x)


def solution(mesh):
    in_specs = (P('dp', 'sp', None, None), P('dp', None, None), P('dp', None), P('dp', None)) + (P(),) * 21
    out_specs = P('dp', 'sp', None, None)
    n = mesh.shape['sp']

    def device_fn(tokens, caption, cap_valid, time_emb, *weights):
        b, rows, width, d = tokens.shape
        assert b == n
        x = exchange(tokens.reshape(b, rows * width, d), 'sp', 0)
        y = image_core(x.reshape(b * rows * width, d), caption, cap_valid, time_emb, 'sp', width, *weights)
        return exchange(y.reshape(b, rows * width, d), 'sp', 1).reshape(tokens.shape)

    return jax.shard_map(device_fn, mesh=mesh, in_specs=in_specs, out_specs=out_specs, check_vma=False)
```

time: 676 us -> 231 us (0.34); the launches traced: 665 us -> 231 us
  matrix products: 294 us -> 0 us
  Pallas kernels: 0 us -> 226 us
  local copies, waits for them, and re-layouts: 160 us -> 4.66 us
  waiting for transfers between devices: 151 us -> 0 us
  other arithmetic: 45.2 us -> 0 us
  between operations: 14.3 us -> 0.03 us
    dot_general x23 -> x0, matrix products: 257 us -> none  [the longest x16 159 us: linear(): jnp.dot(activations, weight, preferred_element_type=jnp.float32)]
    pallas_call x0 -> x3, Pallas kernels: none -> 226 us  [the longest x1 158 us: image_core(): pl.pallas_call(functools.partial(mega_kernel, axis=axis, width=width), in...]
    all_gather x2 -> x0, waiting for transfers between devices: 151 us -> none  [device_fn(): key_vals = lax.all_gather(local_kv, 'sp', axis=1, tiled=True)]
    slice x13 -> x0, local copies, waits for them, and re-layouts: 117 us -> none  [the longest x4 65.1 us: device_fn(): key_vals[:, :, :model_dim]]
    squeeze x4 -> x0, local copies, waits for them, and re-layouts: 39.4 us -> none  [attend(): out_blocks = lax.map(one_block, query_blocks)]
    sub x1 -> x0, matrix products: 37 us -> none  [one_block(): attn_probs = jax.nn.softmax(scores, axis=-1).astype(jnp.bfloat16)]
    sub x3 -> x0, other arithmetic: 22.5 us -> none  [one_block(): attn_probs = jax.nn.softmax(scores, axis=-1).astype(jnp.bfloat16)]
    reduce_sum x11 -> x0, other arithmetic: 12.9 us -> none  [the longest x2 5.97 us: compress(): jnp.sum(grid_view * conv_w.astype(jnp.float32)[:, None, :, :], axis=(2, 4))]
  transfers between devices with their start and end apart: 2 -> 0, of which waited for: 2 -> 0; matrix products, arithmetic and copies ran while one was open for 12% -> 0% of each run, Pallas kernels for 0% -> 0%
where the time goes in v2:
time: 231 us
  Pallas kernels  226 us (98%)
  local copies, waits for them, and re-layouts  4.66 us (2%)
    pallas_call x1, Pallas kernels, image_core(): pl.pallas_call(functools.partial(mega_kernel, axis=axis, width=width), in...  158 us
    pallas_call x2, Pallas kernels, exchange(): pl.pallas_call(functools.partial(exchange_kernel, axis=axis), in_specs=[p...  67.7 us
    unnamed x2, local copies, waits for them, and re-layouts  4.66 us

profile of v2, /device:TPU:81, one launch (start us, length us, event | category | flops | bytes accessed | tf_op | source)
XLA Modules:
  0.0 230.5 jit_solution(16722569572711912415)
XLA Ops:
  0.0 1.4 copy.26.refs_4_
  1.4 35.0 %exchange0.1 = bf16[8,128,1152]{2,1,0:T(8,128)(2,1)} custom-call(bf16[8,128,1152]{2,1,0:T(8,128)(2,1)} %bitcast.7), custom_call_target="tpu_custom_call" | custom-call | tf_op jit(solution)/shard_map/exchange0/pallas_call | solution.py:325
  36.4 158.2 %blocks.1 = bf16[1024,1152]{1,0:T(8,128)(2,1)} custom-call(bf16[1024,1152]{1,0:T(8,128)(2,1)} %bitcast.5, bf16[8,120,1152]{2,1,0:T(8,128)(2,1)} %refs_1_.1, s32[8,120]{1,0:T(8,128)} %refs_2_.1, bf16[8,6912]{1,0:T(8,128)(2,1)} %refs_3_.1, bf16[2,6,1152]{2,1,0:T(8,128)(2,1)} %copy.26.refs_4_, bf16[2,1152]{1,0:T(2,128)(2,1)} %refs_5_.1, ...), custom_call_target="tpu_custom_call" | custom-call | tf_op jit(solution)/shard_map/blocks/pallas_call | solution.py:295
  194.6 32.6 %exchange1.1 = bf16[8,128,1152]{2,1,0:T(8,128)(2,1)} custom-call(bf16[8,128,1152]{2,1,0:T(8,128)(2,1)} %bitcast.4), custom_call_target="tpu_custom_call" | custom-call | tf_op jit(solution)/shard_map/exchange1/pallas_call | solution.py:325
  227.2 3.3 %copy.28 = bf16[8,2,64,1152]{3,2,1,0:T(8,128)(2,1)} copy(bf16[8,2,64,1152]{3,2,1,0:T(8,128)(2,1)} %bitcast.6) | data formatting | bytes 4718592

commit v3 on v2

--- a/solution.py
+++ b/solution.py
@@ -84,13 +84,42 @@
     (x_hbm, cap_hbm, valid_ref, te_ref, tab_ref, bq_ref, bkv_ref, bo_ref, cw_ref, cb_ref, g_ref, gb_ref, cbq_ref, cbkv_ref, cbo_ref, b1_ref, b2_ref,
      wq_hbm, wkv_hbm, wo_hbm, cwq_hbm, cwkv_hbm, cwo_hbm, w1_hbm, w2_hbm, out_hbm,
      wq, wkv, wo, cwq, cwo, w1, w2, x_scr, q_scr, k_scr, vt_scr, kc_scr, vc_scr, cap_scr, vb_scr, bias_scr, mods, sa, sb, sc, sd, ot, h_scr, u_scr, c_scr,
-     wsem, csem, xsem, capsem, osem) = refs
+     wsem, csem, capsem, in_send, in_recv, out_send, out_recv, own_sem) = refs
     t, d = x_scr.shape
     heads = q_scr.shape[0]
     f = w1.shape[1]
     nkeys0 = t // 4
     ncap = kc_scr.shape[2]
+    n, rows_dev = x_hbm.shape[0], x_hbm.shape[1]
+    per_chip = CH // rows_dev
+    chips = n // per_chip
     img = lax.axis_index(axis)
+    my_chip = img // per_chip
+    me = img
+
+    def dev_rows(p):
+        return pl.ds(pl.multiple_of(p * rows_dev, rows_dev), rows_dev)
+
+    def in_copy(p):
+        return pltpu.make_async_remote_copy(src_ref=x_hbm.at[p], dst_ref=x_scr.at[dev_rows(me)], send_sem=in_send.at[p], recv_sem=in_recv.at[me],
+                                            device_id={axis: p}, device_id_type=pl.DeviceIdType.MESH)
+
+    def out_copy(p):
+        return pltpu.make_async_remote_copy(src_ref=x_scr.at[dev_rows(p)], dst_ref=out_hbm.at[me], send_sem=out_send.at[p], recv_sem=out_recv.at[me],
+                                            device_id={axis: p}, device_id_type=pl.DeviceIdType.MESH)
+
+    def ring(k):
+        return lax.rem(my_chip + k, chips)
+
+    def in_chip(c):
+        return ring(lax.rem(c + c // 2 + 2 * (c // 3), chips))
+
+    def out_chip(c):
+        return ring(lax.rem(10 - c + 3 * (c // 2) + 2 * (c // 3), chips))
+
+    barrier = pltpu.get_barrier_semaphore()
+    for k in range(1, n):
+        pl.semaphore_signal(barrier, inc=1, device_id={axis: lax.rem(me + k, n)}, device_id_type=pl.DeviceIdType.MESH)
     hbm = dict(zip(WEIGHTS, (wq_hbm, wkv_hbm, wo_hbm, cwq_hbm, cwo_hbm, w1_hbm, w2_hbm)))
     buf = dict(zip(WEIGHTS, (wq, wkv, wo, cwq, cwo, w1, w2)))
 
@@ -109,13 +138,19 @@
 
     capcopy = pltpu.make_async_copy(cap_hbm.at[img], cap_scr.at[pl.ds(0, cap_hbm.shape[1])], capsem)
     ccopies = [pltpu.make_async_copy(cwkv_hbm.at[l], w1.at[:, pl.ds(l * 2 * d, 2 * d)], csem.at[l]) for l in range(2)]
-    xcopies = [pltpu.make_async_copy(x_hbm.at[pl.ds(c * CH, CH)], x_scr.at[pl.ds(c * CH, CH)], xsem.at[c]) for c in range(t // CH)]
+    own_in = pltpu.make_async_copy(x_hbm.at[me], x_scr.at[dev_rows(me)], own_sem.at[0])
+    own_out = pltpu.make_async_copy(x_scr.at[dev_rows(me)], out_hbm.at[me], own_sem.at[1])
+    own_in.start()
+    partner = me + 1 - 2 * lax.rem(me, per_chip)
     cap_scr[cap_hbm.shape[1]:, :] = jnp.zeros((ncap - cap_hbm.shape[1], d), BF16)
     capcopy.start()
     for c in ccopies:
         c.start()
-    for c in xcopies:
-        c.start()
+    pl.semaphore_wait(barrier, n - 1)
+    in_copy(partner).start()
+    for k in (1, 3, 2):
+        for j in range(per_chip):
+            in_copy(ring(k) * per_chip + j).start()
     for name in ('wq', 'wkv', 'wo', 'cwq', 'cwo', 'w2'):
         wstart(name, 0)
 
@@ -158,10 +193,24 @@
     wstart('w1', 0)
 
     wwait('wq', 0)
-    for c in xcopies:
-        c.wait()
-
-    def prep0(c, _):
+
+    def wait_in(p):
+        pltpu.make_async_remote_copy(src_ref=x_hbm.at[p], dst_ref=x_scr.at[dev_rows(p)], send_sem=in_send.at[p], recv_sem=in_recv.at[p],
+                                     device_id={axis: p}, device_id_type=pl.DeviceIdType.MESH).wait_recv()
+
+    def prep0(step, _):
+        c = in_chip(step)
+
+        @pl.when(step == 0)
+        def _():
+            own_in.wait()
+            wait_in(partner)
+
+        @pl.when(step > 0)
+        def _():
+            for j in range(per_chip):
+                wait_in(c * per_chip + j)
+
         rows = pl.ds(pl.multiple_of(c * CH, CH), CH)
         u = modulate(x_scr[rows, :].astype(F32), 0, 0)
         store_heads(q_scr, rows, (dotf(u, wq[...]) + row(bq_ref, 0)).astype(BF16))
@@ -187,6 +236,10 @@
 
     lax.fori_loop(0, t // CH, prep0, 0)
     wstart('wq', 1)
+    in_copy(partner).wait_send()
+    for k in (1, 3, 2):
+        for j in range(per_chip):
+            in_copy(ring(k) * per_chip + j).wait_send()
     wwait('wkv', 0)
     store_heads(k_scr, slice(0, nkeys0), (dotf(c_scr[...], wkv[:, :d]) + bkv_ref[0:1, :d].astype(F32)).astype(BF16))
     store_heads_t(vt_scr, slice(0, nkeys0), dotf(c_scr[...], wkv[:, d:]) + bkv_ref[0:1, d:].astype(F32))
@@ -198,7 +251,7 @@
         halves = tq // CH
 
         def chunk(c, _):
-            base = pl.multiple_of(c * tq, tq)
+            base = pl.multiple_of((c if layer == 0 else out_chip(c)) * tq, tq)
             rows = pl.ds(base, tq)
             half = [pl.ds(pl.multiple_of(base + i * CH, CH), CH) for i in range(halves)]
 
@@ -253,8 +306,15 @@
             last_use('w1')
             last_use('w2')
             if layer == 1:
-                for i in range(halves):
-                    pltpu.make_async_copy(x_scr.at[half[i]], out_hbm.at[half[i]], osem).start()
+                @pl.when(c < last)
+                def _():
+                    for j in range(per_chip):
+                        out_copy(out_chip(c) * per_chip + j).start()
+
+                @pl.when(c == last)
+                def _():
+                    out_copy(partner).start()
+                    own_out.start()
             return 0
 
         lax.fori_loop(0, t // tq, chunk, 0)
@@ -274,11 +334,21 @@
 
     lax.fori_loop(0, t // CH, prep1, 0)
     tail(1, CH, t, sa, sb, 2)
-    pltpu.make_async_copy(x_scr, out_hbm, osem).wait()
+
+    def wait_out(p):
+        pltpu.make_async_remote_copy(src_ref=x_scr.at[dev_rows(p)], dst_ref=out_hbm.at[p], send_sem=out_send.at[p], recv_sem=out_recv.at[p],
+                                     device_id={axis: p}, device_id_type=pl.DeviceIdType.MESH).wait_recv()
+
+    own_out.wait()
+    for k in range(1, n):
+        p = lax.rem(me + k, n)
+        out_copy(p).wait_send()
+        wait_out(p)
 
 
 def image_core(x, caption, cap_valid, time_emb, axis, width, ada_table, attn_wq, attn_bq, attn_wkv, attn_bkv, attn_wo, attn_bo, comp_w, comp_b, cnorm_g, cnorm_b, cross_wq, cross_bq, cross_wkv, cross_bkv, cross_wo, cross_bo, mlp_w1, mlp_b1, mlp_w2, mlp_b2):
-    t, d = x.shape
+    n, rows_dev, d = x.shape
+    t = n * rows_dev
     f = mlp_w1.shape[2]
     heads = d // HEAD_DIM
     ncap = -(-caption.shape[1] // 128) * 128
@@ -291,45 +361,14 @@
                V((2, heads, ncap, HEAD_DIM), BF16), V((2, heads, HEAD_DIM, ncap), BF16), V((ncap, d), BF16), V((8, ncap), F32), V((ncap, 1), F32), V((2, 6, d), F32),
                V((t, CH), F32), V((t, CH), F32), V((t // 4, 2 * CH), F32), V((t // 4, 2 * CH), F32), V((heads, HEAD_DIM, 2 * CH), F32), V((CH, f), BF16),
                V((d // 128, CH, 128), F32), V((t // 4, d), BF16),
-               pltpu.SemaphoreType.DMA((len(WEIGHTS), SLABS)), pltpu.SemaphoreType.DMA((2,)), pltpu.SemaphoreType.DMA((t // CH,)), pltpu.SemaphoreType.DMA, pltpu.SemaphoreType.DMA]
+               pltpu.SemaphoreType.DMA((len(WEIGHTS), SLABS)), pltpu.SemaphoreType.DMA((2,)), pltpu.SemaphoreType.DMA] + [pltpu.SemaphoreType.DMA((n,))] * 4 + [pltpu.SemaphoreType.DMA((2,))]
     return pl.pallas_call(
         functools.partial(mega_kernel, axis=axis, width=width),
         in_specs=[anyspec, anyspec] + [pl.BlockSpec(memory_space=V)] * len(vmem) + [anyspec] * len(weights),
-        out_specs=anyspec, out_shape=jax.ShapeDtypeStruct((t, d), BF16), scratch_shapes=scratch,
-        compiler_params=pltpu.CompilerParams(vmem_limit_bytes=VLIM),
+        out_specs=anyspec, out_shape=jax.ShapeDtypeStruct(x.shape, BF16), scratch_shapes=scratch,
+        compiler_params=pltpu.CompilerParams(collective_id=0, has_side_effects=True, vmem_limit_bytes=VLIM),
         name="blocks",
     )(x, caption, *vmem, *weights)
-
-
-def exchange_kernel(x_ref, o_ref, send_sem, recv_sem, *, axis):
-    n = x_ref.shape[0]
-    me = lax.axis_index(axis)
-    barrier = pltpu.get_barrier_semaphore()
-    for k in range(1, n):
-        pl.semaphore_signal(barrier, inc=1, device_id={axis: lax.rem(me + k, n)}, device_id_type=pl.DeviceIdType.MESH)
-    pl.semaphore_wait(barrier, n - 1)
-    copies = []
-    for k in range(1, n):
-        peer = lax.rem(me + k, n)
-        cp = pltpu.make_async_remote_copy(src_ref=x_ref.at[peer], dst_ref=o_ref.at[me], send_sem=send_sem.at[k - 1], recv_sem=recv_sem.at[k - 1],
-                                          device_id={axis: peer}, device_id_type=pl.DeviceIdType.MESH)
-        cp.start()
-        copies.append(cp)
-    o_ref[me] = x_ref[me]
-    for cp in copies:
-        cp.wait()
-
-
-def exchange(x, axis, cid):
-    n = x.shape[0]
-    return pl.pallas_call(
-        functools.partial(exchange_kernel, axis=axis),
-        in_specs=[pl.BlockSpec(memory_space=pltpu.VMEM)], out_specs=pl.BlockSpec(memory_space=pltpu.VMEM),
-        out_shape=jax.ShapeDtypeStruct(x.shape, x.dtype),
-        scratch_shapes=[pltpu.SemaphoreType.DMA((n - 1,)), pltpu.SemaphoreType.DMA((n - 1,))],
-        compiler_params=pltpu.CompilerParams(collective_id=cid, has_side_effects=True, vmem_limit_bytes=VLIM),
-        name=f"exchange{cid}",
-    )(x)
 
 
 def solution(mesh):
@@ -339,9 +378,7 @@
 
     def device_fn(tokens, caption, cap_valid, time_emb, *weights):
         b, rows, width, d = tokens.shape
-        assert b == n
-        x = exchange(tokens.reshape(b, rows * width, d), 'sp', 0)
-        y = image_core(x.reshape(b * rows * width, d), caption, cap_valid, time_emb, 'sp', width, *weights)
-        return exchange(y.reshape(b, rows * width, d), 'sp', 1).reshape(tokens.shape)
+        assert b == n and n * rows * width == 4 * CH and CH % (rows * width) == 0
+        return image_core(tokens.reshape(b, rows * width, d), caption, cap_valid, time_emb, 'sp', width, *weights).reshape(tokens.shape)
 
     return jax.shard_map(device_fn, mesh=mesh, in_specs=in_specs, out_specs=out_specs, check_vma=False)

time: 231 us -> 176 us (0.76)
  Pallas kernels: 226 us -> 171 us
    pallas_call x2 -> x0, Pallas kernels: 67.7 us -> none  [exchange(): pl.pallas_call(functools.partial(exchange_kernel, axis=axis), in_specs=[p...]
    pallas_call x1, Pallas kernels: 158 us -> 171 us  [image_core(): pl.pallas_call(functools.partial(mega_kernel, axis=axis, width=width), in...]
where the time goes in v3:
time: 176 us
  Pallas kernels  171 us (97%)
  local copies, waits for them, and re-layouts  4.67 us (3%)
    pallas_call x1, Pallas kernels, image_core(): pl.pallas_call(functools.partial(mega_kernel, axis=axis, width=width), in...  171 us
    unnamed x2, local copies, waits for them, and re-layouts  4.67 us

profile of v3, /device:TPU:81, one launch (start us, length us, event | category | flops | bytes accessed | tf_op | source)
XLA Modules:
  0.0 175.8 jit_solution(8739996613516088832)
XLA Ops:
  0.0 1.4 copy.26.refs_4_
  1.4 171.2 %blocks.1 = bf16[8,128,1152]{2,1,0:T(8,128)(2,1)} custom-call(bf16[8,128,1152]{2,1,0:T(8,128)(2,1)} %bitcast.3, bf16[8,120,1152]{2,1,0:T(8,128)(2,1)} %refs_1_.1, s32[8,120]{1,0:T(8,128)} %refs_2_.1, bf16[8,6912]{1,0:T(8,128)(2,1)} %refs_3_.1, bf16[2,6,1152]{2,1,0:T(8,128)(2,1)} %copy.26.refs_4_, bf16[2,1152]{1,0:T(2,128)(2,1)} %refs_5_.1, ...), custom_call_target="tpu_custom_call" | custom-call | tf_op jit(solution)/shard_map/blocks/pallas_call | solution.py:365
  172.5 3.3 %copy.28 = bf16[8,2,64,1152]{3,2,1,0:T(8,128)(2,1)} copy(bf16[8,2,64,1152]{3,2,1,0:T(8,128)(2,1)} %bitcast.2) | data formatting | bytes 4718592

commit v4 on v3

--- a/solution.py
+++ b/solution.py
@@ -10,7 +10,7 @@
 LN_EPS = 1e-6
 F32, BF16 = jnp.float32, jnp.bfloat16
 SM_SCALE = HEAD_DIM ** -0.5 * math.log2(math.e)
-VLIM = 66_900_000
+VLIM = 64_500_000
 CH = 256
 WEIGHTS = ('wq', 'wkv', 'wo', 'cwq', 'cwo', 'w1', 'w2')
 SLABS = 4
@@ -38,52 +38,60 @@
     return op(v.reshape(v.shape[0] // 8, 8, v.shape[1]), axis=0)
 
 
-def attention(q_at, k_at, v_at, ot_ref, sa, sb, nb, kb_size, heads, bias_at, unroll):
+def attention(q_at, k_at, v_at, ot_ref, sa, sb, nb, kb_size, heads, bias_at, unroll, group=1):
+    nkeys = nb * kb_size
+
     def scores(h, kb, q):
         s = lax.dot_general(k_at(h, kb), q, (((1,), (1,)), ((), ())), preferred_element_type=F32)
         return s if bias_at is None else s + bias_at(kb)
 
+    def form(h, kb, g, q, dst, mx):
+        s = scores(h, kb, q)
+        dst[g * nkeys + kb * kb_size:g * nkeys + (kb + 1) * kb_size, :] = s
+        f = fold(s, jnp.max)
+        return f if mx is None else jnp.maximum(mx, f)
+
     def first():
-        q = q_at(0)
-        mx = None
-        for kb in range(nb):
-            s = scores(0, kb, q)
-            sa[kb * kb_size:(kb + 1) * kb_size, :] = s
-            f = fold(s, jnp.max)
-            mx = f if mx is None else jnp.maximum(mx, f)
-        return mx
-
-    def step(h, hn, mx, cur, nxt):
-        m = jnp.max(mx, axis=0, keepdims=True)
-        q = q_at(hn)
-        mn = l = acc = None
-        for kb in range(nb):
-            sl = slice(kb * kb_size, (kb + 1) * kb_size)
-            s = scores(hn, kb, q)
-            nxt[sl, :] = s
-            f = fold(s, jnp.max)
-            mn = f if mn is None else jnp.maximum(mn, f)
-            e = jnp.exp2((cur[sl, :] - m) * SM_SCALE)
-            f = fold(e, jnp.sum)
-            l = f if l is None else l + f
-            a = dotf(v_at(h, kb), e.astype(BF16))
-            acc = a if acc is None else acc + a
-        l = jnp.sum(l, axis=0, keepdims=True)
-        ot_ref[h] = acc * (1.0 / l)
-        return mn
-
-    def body(i, mx):
-        h = 2 * i
-        mx = step(h, h + 1, mx, sa, sb)
-        return step(h + 1, jnp.minimum(h + 2, heads - 1), mx, sb, sa)
-
-    lax.fori_loop(0, heads // 2, body, first(), unroll=unroll)
+        out = []
+        for g in range(group):
+            q = q_at(g)
+            mx = None
+            for kb in range(nb):
+                mx = form(g, kb, g, q, sa, mx)
+            out.append(mx)
+        return tuple(out)
+
+    def step(i, inext, mxs, cur, nxt):
+        out = []
+        for g in range(group):
+            h, hn = i * group + g, inext * group + g
+            m = jnp.max(mxs[g], axis=0, keepdims=True)
+            q = q_at(hn)
+            mn = l = acc = None
+            for kb in range(nb):
+                mn = form(hn, kb, g, q, nxt, mn)
+                e = jnp.exp2((cur[g * nkeys + kb * kb_size:g * nkeys + (kb + 1) * kb_size, :] - m) * SM_SCALE)
+                f = fold(e, jnp.sum)
+                l = f if l is None else l + f
+                a = dotf(v_at(h, kb), e.astype(BF16))
+                acc = a if acc is None else acc + a
+            l = jnp.sum(l, axis=0, keepdims=True)
+            ot_ref[h] = acc * (1.0 / l)
+            out.append(mn)
+        return tuple(out)
+
+    def body(j, mxs):
+        i = 2 * j
+        mxs = step(i, i + 1, mxs, sa, sb)
+        return step(i + 1, jnp.minimum(i + 2, heads // group - 1), mxs, sb, sa)
+
+    lax.fori_loop(0, heads // group // 2, body, first(), unroll=unroll)
 
 
 def mega_kernel(*refs, axis, width):
     (x_hbm, cap_hbm, valid_ref, te_ref, tab_ref, bq_ref, bkv_ref, bo_ref, cw_ref, cb_ref, g_ref, gb_ref, cbq_ref, cbkv_ref, cbo_ref, b1_ref, b2_ref,
      wq_hbm, wkv_hbm, wo_hbm, cwq_hbm, cwkv_hbm, cwo_hbm, w1_hbm, w2_hbm, out_hbm,
-     wq, wkv, wo, cwq, cwo, w1, w2, x_scr, q_scr, k_scr, vt_scr, kc_scr, vc_scr, cap_scr, vb_scr, bias_scr, mods, sa, sb, sc, sd, ot, h_scr, u_scr, c_scr,
+     wqkv, wo, cwq, cwo, w1, w2, x_scr, q_scr, k_scr, vt_scr, kc_scr, vc_scr, vb_scr, bias_scr, mods, sa, sb, sc, sd, ot, h_scr, u_scr,
      wsem, csem, capsem, in_send, in_recv, out_send, out_recv, own_sem) = refs
     t, d = x_scr.shape
     heads = q_scr.shape[0]
@@ -121,6 +129,8 @@
     for k in range(1, n):
         pl.semaphore_signal(barrier, inc=1, device_id={axis: lax.rem(me + k, n)}, device_id_type=pl.DeviceIdType.MESH)
     hbm = dict(zip(WEIGHTS, (wq_hbm, wkv_hbm, wo_hbm, cwq_hbm, cwo_hbm, w1_hbm, w2_hbm)))
+    cap_scr, c_scr = h_scr.at[:ncap, 2 * d:3 * d], h_scr.at[:, :d]
+    wq, wkv = wqkv.at[:, :d], wqkv.at[:, d:]
     buf = dict(zip(WEIGHTS, (wq, wkv, wo, cwq, cwo, w1, w2)))
 
     def wcopies(name, layer):
@@ -215,17 +225,16 @@
         u = modulate(x_scr[rows, :].astype(F32), 0, 0)
         store_heads(q_scr, rows, (dotf(u, wq[...]) + row(bq_ref, 0)).astype(BF16))
         uf = u.astype(F32)
-        for j in range(d // 128):
-            u_scr[j] = uf[:, j * 128:(j + 1) * 128]
         parts = []
         for r in range(CH // width // 2):
             cols = []
             for j in range(d // 128):
+                u_scr[j] = uf[2 * r * width:2 * (r + 1) * width, j * 128:(j + 1) * 128]
                 acc = None
                 for a in range(2):
                     for b in range(2):
                         w = cw_ref[a, b:b + 1, j * 128:(j + 1) * 128].astype(F32)
-                        v = u_scr[j, pl.ds((2 * r + a) * width + b, width // 2, stride=2), :] * w
+                        v = u_scr[j, pl.ds(a * width + b, width // 2, stride=2), :] * w
                         acc = v if acc is None else acc + v
                 cols.append(acc)
             parts.append(jnp.concatenate(cols, axis=1))
@@ -241,11 +250,14 @@
         for j in range(per_chip):
             in_copy(ring(k) * per_chip + j).wait_send()
     wwait('wkv', 0)
-    store_heads(k_scr, slice(0, nkeys0), (dotf(c_scr[...], wkv[:, :d]) + bkv_ref[0:1, :d].astype(F32)).astype(BF16))
-    store_heads_t(vt_scr, slice(0, nkeys0), dotf(c_scr[...], wkv[:, d:]) + bkv_ref[0:1, d:].astype(F32))
+    y = dotf(c_scr[...], wkv[...]) + row(bkv_ref, 0)
+    store_heads(k_scr, slice(0, nkeys0), y[:, :d].astype(BF16))
+    store_heads_t(vt_scr, slice(0, nkeys0), y[:, d:])
     wstart('wkv', 1)
 
-    def tail(layer, tq, nkeys, sx, sy, unroll):
+    def tail(layer, tq, nkeys, sx, sy, unroll, cg):
+        for name in ('wo', 'cwq', 'cwo', 'w1', 'w2'):
+            wwait(name, layer)
         last = t // tq - 1
         kb = min(nkeys, 256)
         halves = tq // CH
@@ -255,38 +267,19 @@
             rows = pl.ds(base, tq)
             half = [pl.ds(pl.multiple_of(base + i * CH, CH), CH) for i in range(halves)]
 
-            def first_use(name):
-                @pl.when(c == 0)
-                def _():
-                    wwait(name, layer)
-
-            def last_use(name):
-                if layer == 0:
-                    @pl.when(c == last)
-                    def _():
-                        wstart(name, 1)
-
             attention(lambda h: q_scr[h, rows, :], lambda h, i: k_scr[h, i * kb:(i + 1) * kb, :], lambda h, i: vt_scr[h, :, i * kb:(i + 1) * kb],
                       ot.at[:, :, :tq], sx, sy, nkeys // kb, kb, heads, None, unroll)
-            first_use('wo')
-            first_use('cwq')
             for i in range(halves):
                 o = ot[:, :, i * CH:(i + 1) * CH].reshape(d, CH).T.astype(BF16)
                 x = x_scr[half[i], :].astype(F32)
                 x = (x + mods[layer, 2:3, :] * (dotf(o, wo[...]) + row(bo_ref, layer))).astype(BF16)
                 x_scr[half[i], :] = x
                 store_heads(q_scr, half[i], (dotf(x, cwq[...]) + row(cbq_ref, layer)).astype(BF16))
-            last_use('wo')
-            last_use('cwq')
             attention(lambda h: q_scr[h, rows, :], lambda h, i: kc_scr[layer, h], lambda h, i: vc_scr[layer, h],
-                      ot.at[:, :, :tq], sc.at[:, :tq], sd.at[:, :tq], 1, ncap, heads, lambda i: bias_scr[...], 8)
-            first_use('cwo')
+                      ot.at[:, :, :tq], sx, sy, 1, ncap, heads, lambda i: bias_scr[...], heads // cg // 2, cg)
             for i in range(halves):
                 o = ot[:, :, i * CH:(i + 1) * CH].reshape(d, CH).T.astype(BF16)
                 x_scr[half[i], :] = (x_scr[half[i], :].astype(F32) + (dotf(o, cwo[...]) + row(cbo_ref, layer))).astype(BF16)
-            last_use('cwo')
-            first_use('w1')
-            first_use('w2')
 
             def mlp(i, _):
                 r = pl.ds(pl.multiple_of(base + i * CH, CH), CH)
@@ -303,8 +296,6 @@
                 mlp(0, 0)
             else:
                 lax.fori_loop(0, halves, mlp, 0)
-            last_use('w1')
-            last_use('w2')
             if layer == 1:
                 @pl.when(c < last)
                 def _():
@@ -319,7 +310,9 @@
 
         lax.fori_loop(0, t // tq, chunk, 0)
 
-    tail(0, 2 * CH, nkeys0, sc, sd, 4)
+    tail(0, 2 * CH, nkeys0, sc, sd, 4, 2)
+    for name in ('wo', 'cwq', 'cwo', 'w1', 'w2'):
+        wstart(name, 1)
 
     wwait('wq', 1)
     wwait('wkv', 1)
@@ -327,13 +320,14 @@
     def prep1(c, _):
         rows = pl.ds(pl.multiple_of(c * CH, CH), CH)
         u = modulate(x_scr[rows, :].astype(F32), 1, 0)
-        store_heads(q_scr, rows, (dotf(u, wq[...]) + row(bq_ref, 1)).astype(BF16))
-        store_heads(k_scr, rows, (dotf(u, wkv[:, :d]) + bkv_ref[1:2, :d].astype(F32)).astype(BF16))
-        store_heads_t(vt_scr, rows, dotf(u, wkv[:, d:]) + bkv_ref[1:2, d:].astype(F32))
+        y = dotf(u, wqkv[...])
+        store_heads(q_scr, rows, (y[:, :d] + row(bq_ref, 1)).astype(BF16))
+        store_heads(k_scr, rows, (y[:, d:2 * d] + bkv_ref[1:2, :d].astype(F32)).astype(BF16))
+        store_heads_t(vt_scr, rows, y[:, 2 * d:] + bkv_ref[1:2, d:].astype(F32))
         return 0
 
     lax.fori_loop(0, t // CH, prep1, 0)
-    tail(1, CH, t, sa, sb, 2)
+    tail(1, CH, t, sa, sb, 4, 4)
 
     def wait_out(p):
         pltpu.make_async_remote_copy(src_ref=x_scr.at[dev_rows(p)], dst_ref=out_hbm.at[p], send_sem=out_send.at[p], recv_sem=out_recv.at[p],
@@ -356,16 +350,16 @@
     weights = [attn_wq, attn_wkv, attn_wo, cross_wq, cross_wkv, cross_wo, mlp_w1, mlp_w2]
     anyspec = pl.BlockSpec(memory_space=pl.ANY)
     V = pltpu.VMEM
-    scratch = [V((d, d), BF16), V((d, 2 * d), BF16), V((d, d), BF16), V((d, d), BF16), V((d, d), BF16), V((d, f), BF16), V((f, d), BF16),
+    scratch = [V((d, 3 * d), BF16), V((d, d), BF16), V((d, d), BF16), V((d, d), BF16), V((d, f), BF16), V((f, d), BF16),
                V((t, d), BF16), V((heads, t, HEAD_DIM), BF16), V((heads, t, HEAD_DIM), BF16), V((heads, HEAD_DIM, t), BF16),
-               V((2, heads, ncap, HEAD_DIM), BF16), V((2, heads, HEAD_DIM, ncap), BF16), V((ncap, d), BF16), V((8, ncap), F32), V((ncap, 1), F32), V((2, 6, d), F32),
+               V((2, heads, ncap, HEAD_DIM), BF16), V((2, heads, HEAD_DIM, ncap), BF16), V((8, ncap), F32), V((ncap, 1), F32), V((2, 6, d), F32),
                V((t, CH), F32), V((t, CH), F32), V((t // 4, 2 * CH), F32), V((t // 4, 2 * CH), F32), V((heads, HEAD_DIM, 2 * CH), F32), V((CH, f), BF16),
-               V((d // 128, CH, 128), F32), V((t // 4, d), BF16),
+               V((d // 128, 2 * width, 128), F32),
                pltpu.SemaphoreType.DMA((len(WEIGHTS), SLABS)), pltpu.SemaphoreType.DMA((2,)), pltpu.SemaphoreType.DMA] + [pltpu.SemaphoreType.DMA((n,))] * 4 + [pltpu.SemaphoreType.DMA((2,))]
     return pl.pallas_call(
         functools.partial(mega_kernel, axis=axis, width=width),
         in_specs=[anyspec, anyspec] + [pl.BlockSpec(memory_space=V)] * len(vmem) + [anyspec] * len(weights),
-        out_specs=anyspec, out_shape=jax.ShapeDtypeStruct(x.shape, BF16), scratch_shapes=scratch,
+        out_specs=pl.BlockSpec(memory_space=V), out_shape=V(x.shape, BF16), scratch_shapes=scratch,
         compiler_params=pltpu.CompilerParams(collective_id=0, has_side_effects=True, vmem_limit_bytes=VLIM),
         name="blocks",
     )(x, caption, *vmem, *weights)

time: 176 us -> 163 us (0.926)
  Pallas kernels: 171 us -> 160 us
  local copies, waits for them, and re-layouts: 4.67 us -> 2.77 us
    pallas_call x1, Pallas kernels: 171 us -> 160 us  [image_core(): pl.pallas_call(functools.partial(mega_kernel, axis=axis, width=width), in...]
    unnamed x2, local copies, waits for them, and re-layouts: 4.67 us -> 2.77 us
where the time goes in v4:
time: 163 us
  Pallas kernels  160 us (98%)
  local copies, waits for them, and re-layouts  2.77 us (2%)
    pallas_call x1, Pallas kernels, image_core(): pl.pallas_call(functools.partial(mega_kernel, axis=axis, width=width), in...  160 us

profile of v4, /device:TPU:81, one launch (start us, length us, event | category | flops | bytes accessed | tf_op | source)
XLA Modules:
  0.0 163.0 jit_solution(4272968880473658639)
XLA Ops:
  0.0 1.4 copy.26.refs_4_
  1.4 160.3 %blocks.1 = bf16[8,128,1152]{2,1,0:T(8,128)(2,1)S(1)} custom-call(bf16[8,128,1152]{2,1,0:T(8,128)(2,1)} %bitcast.3, bf16[8,120,1152]{2,1,0:T(8,128)(2,1)} %refs_1_.1, s32[8,120]{1,0:T(8,128)} %refs_2_.1, bf16[8,6912]{1,0:T(8,128)(2,1)} %refs_3_.1, bf16[2,6,1152]{2,1,0:T(8,128)(2,1)} %copy.26.refs_4_, bf16[2,1152]{1,0:T(2,128)(2,1)} %refs_5_.1, ...), custom_call_target="tpu_custom_call" | custom-call | tf_op jit(solution)/shard_map/blocks/pallas_call | solution.py:359
  161.6 1.4 copy.28

commit v5 on v4

--- a/solution.py
+++ b/solution.py
@@ -168,7 +168,7 @@
     te = jnp.sum(jnp.where(pick, te_ref[...].astype(F32), 0.0), axis=0, keepdims=True)
     for l in range(2):
         for j in range(6):
-            mods[l, j:j + 1, :] = te[:, j * d:(j + 1) * d] + tab_ref[l, j:j + 1, :].astype(F32)
+            mods[l, j:j + 1, :] = te[:, j * d:(j + 1) * d] + tab_ref[j, l:l + 1, :].astype(F32)
     vb_scr[...] = jnp.full(vb_scr.shape, -jnp.inf, F32)
     valid = jnp.sum(jnp.where(pick, valid_ref[...], 0), axis=0, keepdims=True)
     vb = jnp.where(valid > 0, 0.0, -1e9 / HEAD_DIM ** -0.5).astype(F32)
@@ -267,8 +267,17 @@
             rows = pl.ds(base, tq)
             half = [pl.ds(pl.multiple_of(base + i * CH, CH), CH) for i in range(halves)]
 
-            attention(lambda h: q_scr[h, rows, :], lambda h, i: k_scr[h, i * kb:(i + 1) * kb, :], lambda h, i: vt_scr[h, :, i * kb:(i + 1) * kb],
-                      ot.at[:, :, :tq], sx, sy, nkeys // kb, kb, heads, None, unroll)
+            if layer == 0:
+                def self_half(i, _):
+                    r = pl.ds(pl.multiple_of(base + i * CH, CH), CH)
+                    attention(lambda h: q_scr[h, r, :], lambda h, j: k_scr[h, j * kb:(j + 1) * kb, :], lambda h, j: vt_scr[h, :, j * kb:(j + 1) * kb],
+                              ot.at[:, :, pl.ds(pl.multiple_of(i * CH, CH), CH)], sa, sb, nkeys // kb, kb, heads, None, 1, 4)
+                    return 0
+
+                lax.fori_loop(0, halves, self_half, 0)
+            else:
+                attention(lambda h: q_scr[h, rows, :], lambda h, i: k_scr[h, i * kb:(i + 1) * kb, :], lambda h, i: vt_scr[h, :, i * kb:(i + 1) * kb],
+                          ot.at[:, :, :tq], sx, sy, nkeys // kb, kb, heads, None, unroll)
             for i in range(halves):
                 o = ot[:, :, i * CH:(i + 1) * CH].reshape(d, CH).T.astype(BF16)
                 x = x_scr[half[i], :].astype(F32)
@@ -327,7 +336,7 @@
         return 0
 
     lax.fori_loop(0, t // CH, prep1, 0)
-    tail(1, CH, t, sa, sb, 4, 4)
+    tail(1, CH, t, sa, sb, 8, 4)
 
     def wait_out(p):
         pltpu.make_async_remote_copy(src_ref=x_scr.at[dev_rows(p)], dst_ref=out_hbm.at[p], send_sem=out_send.at[p], recv_sem=out_recv.at[p],
@@ -346,7 +355,7 @@
     f = mlp_w1.shape[2]
     heads = d // HEAD_DIM
     ncap = -(-caption.shape[1] // 128) * 128
-    vmem = [cap_valid, time_emb, ada_table, attn_bq, attn_bkv, attn_bo, comp_w, comp_b, cnorm_g, cnorm_b, cross_bq, cross_bkv, cross_bo, mlp_b1, mlp_b2]
+    vmem = [cap_valid, time_emb, jnp.swapaxes(ada_table, 0, 1), attn_bq, attn_bkv, attn_bo, comp_w, comp_b, cnorm_g, cnorm_b, cross_bq, cross_bkv, cross_bo, mlp_b1, mlp_b2]
     weights = [attn_wq, attn_wkv, attn_wo, cross_wq, cross_wkv, cross_wo, mlp_w1, mlp_w2]
     anyspec = pl.BlockSpec(memory_space=pl.ANY)
     V = pltpu.VMEM

time: 163 us -> 159 us (0.975)
  Pallas kernels: 160 us -> 157 us
    pallas_call x1, Pallas kernels: 160 us -> 157 us  [image_core(): pl.pallas_call(functools.partial(mega_kernel, axis=axis, width=width), in...]
where the time goes in v5:
time: 159 us
  Pallas kernels  157 us (99%)
    pallas_call x1, Pallas kernels, image_core(): pl.pallas_call(functools.partial(mega_kernel, axis=axis, width=width), in...  157 us

profile of v5, /device:TPU:81, one launch (start us, length us, event | category | flops | bytes accessed | tf_op | source)
XLA Modules:
  0.0 158.6 jit_solution(13161550921398139400)
XLA Ops:
  0.0 157.2 %blocks.1 = bf16[8,128,1152]{2,1,0:T(8,128)(2,1)S(1)} custom-call(bf16[8,128,1152]{2,1,0:T(8,128)(2,1)} %bitcast.4, bf16[8,120,1152]{2,1,0:T(8,128)(2,1)} %refs_1_.1, s32[8,120]{1,0:T(8,128)} %refs_2_.1, bf16[8,6912]{1,0:T(8,128)(2,1)} %refs_3_.1, bf16[6,2,1152]{2,1,0:T(2,128)(2,1)} %bitcast.5, bf16[2,1152]{1,0:T(2,128)(2,1)} %refs_5_.1, ...), custom_call_target="tpu_custom_call" | custom-call | tf_op jit(solution)/shard_map/blocks/pallas_call | solution.py:368
  157.2 1.4 copy.27
